TPU v7x, 32 devices: a whole 2x2x4 slice. The times are simulated.
32 devices in a mesh: sweep: 2 (over y), expert: 4 (over z), dp: 4 (over x, core).
Axes of the slice: x: 2, y: 2, z: 4, core: 2. Of those that a mesh axis runs over, the one named last changes fastest.
Arguments:
- tokens: bfloat16 [4096, 1536], P(('sweep', 'expert', 'dp')), parts along dimension 0, may hold values from -6 to 6
- expert_ids: int32 [4096, 8], P(('sweep', 'expert', 'dp')), parts along dimension 0, may hold values from 0 to 63, all different within a row; in each aligned block of 128 rows (0 to 127, 128 to 255, ...) at most 20 rows name the same one
- gate_weights: float32 [4096, 8], P(('sweep', 'expert', 'dp')), parts along dimension 0, may hold values from 0.1 to 0.6
- expert_in: bfloat16 [128, 1536, 768], P(('sweep', 'expert'), 'dp'), parts along dimension 0, may hold values from -0.15625 to 0.15625
- expert_out: bfloat16 [128, 768, 1536], P(('sweep', 'expert'), None, 'dp'), parts along dimension 0, may hold values from -0.21875 to 0.21875
- shared_in: bfloat16 [3072, 768], P(('sweep', 'dp')), parts along dimension 0, may hold values from -0.15625 to 0.15625
- shared_out: bfloat16 [1536, 1536], P('sweep', 'dp'), parts along dimension 0, may hold values from -0.21875 to 0.21875
Outputs:
- block_out: bfloat16 [4096, 1536], P(('sweep', 'expert', 'dp')), parts along dimension 0
There are 2 independent parts, one for each index of `sweep`. A program takes and returns all parts, laid end to end along the dimension named above; each array names one. Nothing has to cross between parts.
Inputs may be any that keep to these rules, and one draw needn't show every extreme that they name: `expert_ids`: each token names 8 different experts. In each aligned block of 128 tokens (the tokens of one device) no expert is named by more than 20 tokens; some blocks have an expert named by exactly 20.
All inputs are finite; a program needn't handle non-finite values.
Results may differ from a plain program's by a relative error of at most 0.0051.
Values may be sent and summed in bfloat16 or wider, within the bound.
A program may use at most 192 MiB of HBM per device.

v0:
```python
import functools

import jax
import jax.numpy as jnp
from jax import lax
from jax.experimental import pallas as pl
from jax.experimental.pallas import tpu as pltpu
from jax.sharding import PartitionSpec as P

CAP = 20
GROUP = 4


def layer_norm(tokens):
    values = tokens.astype(jnp.float32)
    center = values - jnp.mean(values, axis=-1, keepdims=True)
    spread = jnp.mean(center * center, axis=-1, keepdims=True)
    return (center * lax.rsqrt(spread + 1e-06)).astype(jnp.bfloat16)


def first_kernel(runs, run_tokens, x_ref, key_ref, w_ref, out_ref, rows_ref):
    slots = out_ref.shape[3]
    for j in range(runs):
        span = slice(j * run_tokens, (j + 1) * run_tokens)
        row = lax.broadcasted_iota(jnp.int32, (slots, run_tokens), 0)
        pick = jnp.where(row == key_ref[0, :, span], 1.0, 0.0).astype(jnp.bfloat16)
        rows_ref[j * slots : (j + 1) * slots, :] = jnp.dot(
            pick, x_ref[span, :], preferred_element_type=jnp.float32
        ).astype(jnp.bfloat16)
    pre = jnp.dot(rows_ref[...], w_ref[0], preferred_element_type=jnp.float32)
    for j in range(runs):
        out_ref[j, 0, 0] = pre[j * slots : (j + 1) * slots].astype(jnp.bfloat16)


def first_projection(x, keys, weight, first, count, runs, run_tokens, slots):
    width, hidden = weight.shape[1:]
    chunk = runs * run_tokens
    chunks = x.shape[0] // chunk
    total = count * chunks * runs * slots
    return pl.pallas_call(
        functools.partial(first_kernel, runs, run_tokens),
        grid=(count, chunks),
        in_specs=[
            pl.BlockSpec((chunk, width), lambda e, c: (c, 0)),
            pl.BlockSpec((1, 1, chunk), lambda e, c: (e + first, 0, c)),
            pl.BlockSpec((1, width, hidden), lambda e, c: (e + first, 0, 0)),
        ],
        out_specs=pl.BlockSpec((runs, 1, 1, slots, hidden), lambda e, c: (0, e, c, 0, 0)),
        out_shape=jax.ShapeDtypeStruct((runs, count, chunks, slots, hidden), jnp.bfloat16),
        scratch_shapes=[pltpu.VMEM((runs * slots, width), jnp.bfloat16)],
        cost_estimate=pl.CostEstimate(
            flops=2 * total * width * (hidden + run_tokens),
            bytes_accessed=2 * (count * width * hidden + total * hidden + x.size),
            transcendentals=0,
        ),
    )(x, keys, weight)


def second_kernel(runs, run_tokens, h_ref, key_ref, gate_ref, w_ref, *refs):
    carry_ref, (out_ref, total_ref) = refs[0] if len(refs) == 3 else None, refs[-2:]
    expert = pl.program_id(1)
    slots = h_ref.shape[3]

    @pl.when(expert == 0)
    def _():
        total_ref[...] = jnp.zeros_like(total_ref) if carry_ref is None else carry_ref[...]

    h = jnp.concatenate([h_ref[j, 0, 0] for j in range(runs)], axis=0)
    result = jnp.dot(h, w_ref[0], preferred_element_type=jnp.float32)
    for j in range(runs):
        span = slice(j * run_tokens, (j + 1) * run_tokens)
        row = lax.broadcasted_iota(jnp.int32, (slots, run_tokens), 0)
        match = row == key_ref[0, :, span]
        gate = jnp.sum(jnp.where(match, gate_ref[0, :, span], 0.0), axis=1, keepdims=True)
        scaled = (result[j * slots : (j + 1) * slots] * gate).astype(jnp.bfloat16)
        total_ref[span, :] += lax.dot_general(
            jnp.where(match, 1.0, 0.0).astype(jnp.bfloat16),
            scaled,
            (((0,), (0,)), ((), ())),
            preferred_element_type=jnp.float32,
        )

    @pl.when(expert == pl.num_programs(1) - 1)
    def _():
        out_ref[...] = total_ref[...].astype(out_ref.dtype)


def second_projection(hidden, keys, gates, weight, carry, kind, first, runs, run_tokens):
    _, count, chunks, slots, depth = hidden.shape
    width = weight.shape[2]
    chunk = runs * run_tokens
    total = count * chunks * runs * slots
    carries = [] if carry is None else [carry]
    return pl.pallas_call(
        functools.partial(second_kernel, runs, run_tokens),
        grid=(chunks, count),
        in_specs=[
            pl.BlockSpec((runs, 1, 1, slots, depth), lambda c, e: (0, e, c, 0, 0)),
            pl.BlockSpec((1, 1, chunk), lambda c, e: (e + first, 0, c)),
            pl.BlockSpec((1, 1, chunk), lambda c, e: (e + first, 0, c)),
            pl.BlockSpec((1, depth, width), lambda c, e: (e + first, 0, 0)),
        ]
        + [pl.BlockSpec((chunk, width), lambda c, e: (c, 0)) for _ in carries],
        out_specs=pl.BlockSpec((chunk, width), lambda c, e: (c, 0)),
        out_shape=jax.ShapeDtypeStruct((chunks * chunk, width), kind),
        scratch_shapes=[pltpu.VMEM((chunk, width), jnp.float32)],
        cost_estimate=pl.CostEstimate(
            flops=2 * total * width * (depth + 3 * run_tokens),
            bytes_accessed=2 * (count * depth * width + total * depth) + 4 * chunks * chunk * width,
            transcendentals=0,
        ),
    )(hidden, keys, gates, weight, *carries)


def per_device(tokens, expert_ids, gate_weights, expert_in, expert_out, shared_in, shared_out):
    row_count, model_width = tokens.shape
    pick_count = expert_ids.shape[1]
    local_count = expert_in.shape[0]
    runs = lax.axis_size("dp")
    block_count = runs * lax.axis_size("expert")
    run_tokens = GROUP * row_count
    slots = GROUP * CAP
    halves = 2 if local_count % 2 == 0 else 1

    normed = layer_norm(tokens)
    full_shared_in = lax.all_gather(shared_in, "dp", axis=0, tiled=True)
    full_shared_out = lax.all_gather(shared_out, "dp", axis=1, tiled=True)

    named = jnp.concatenate([expert_ids.astype(jnp.float32), gate_weights], axis=1).T
    named = lax.all_gather(named, ("expert", "dp"), axis=0, tiled=False)
    ids, gates = named[:, :pick_count], named[:, pick_count:]
    columns = lax.all_to_all(normed, "dp", split_axis=1, concat_axis=0, tiled=True)
    columns, full_shared_in, full_shared_out = lax.optimization_barrier(
        (columns, full_shared_in, full_shared_out)
    )
    x = lax.all_gather(columns, "expert", axis=0, tiled=True)

    owned = lax.axis_index("expert") * local_count + jnp.arange(local_count, dtype=jnp.int32)
    matches = ids[:, :, None, :] == owned.astype(jnp.float32)[:, None]
    chosen = jnp.any(matches, axis=1)
    gate_of = jnp.sum(jnp.where(matches, gates[:, :, None, :], 0.0), axis=1)
    order = jnp.arange(row_count, dtype=jnp.int32)
    before = (order[:, None] < order[None, :]).astype(jnp.bfloat16)
    earlier = jnp.einsum(
        "bej,ji->bei", chosen.astype(jnp.bfloat16), before, preferred_element_type=jnp.float32
    ).astype(jnp.int32)
    base = jnp.arange(block_count, dtype=jnp.int32) % GROUP * CAP
    keys = jnp.where(chosen, earlier + base[:, None, None], -1)

    def by_expert(table):
        return table.transpose(1, 0, 2).reshape(local_count, 1, block_count * row_count)

    keys, gate_of = by_expert(keys), by_expert(gate_of)

    count = local_count // halves
    parts = []
    for half in range(halves):
        pre = first_projection(
            x, keys, expert_in, half * count, count, runs, run_tokens, slots
        )
        parts.append(lax.psum_scatter(pre, "dp", scatter_dimension=0, tiled=True))

    hidden = []
    for pre in parts:
        act = jax.nn.gelu(pre.astype(jnp.float32)).astype(jnp.bfloat16)
        hidden.append(lax.all_gather(act, "dp", axis=0, tiled=True))

    shared_pre = jnp.dot(normed, full_shared_in, preferred_element_type=jnp.float32)
    shared_hidden = jax.nn.gelu(shared_pre).astype(jnp.bfloat16)
    shared_result = jnp.dot(shared_hidden, full_shared_out, preferred_element_type=jnp.float32)

    routed = None
    for half, h in enumerate(hidden):
        kind = jnp.bfloat16 if half == halves - 1 else jnp.float32
        routed = second_projection(
            h, keys, gate_of, expert_out, routed, kind, half * count, runs, run_tokens
        )
    width = routed.shape[1]
    pieces = lax.all_to_all(
        routed.reshape(block_count, row_count, width),
        ("expert", "dp"),
        split_axis=0,
        concat_axis=0,
        tiled=True,
    ).reshape(-1, runs, row_count, width)
    own = jnp.sum(pieces.astype(jnp.float32), axis=0).transpose(1, 0, 2)
    own = own.reshape(row_count, model_width)
    return (tokens.astype(jnp.float32) + shared_result + own).astype(jnp.bfloat16)


def solution(mesh):
    placed = (
        P(("sweep", "expert", "dp"), None),
        P(("sweep", "expert", "dp"), None),
        P(("sweep", "expert", "dp"), None),
        P(("sweep", "expert"), "dp", None),
        P(("sweep", "expert"), None, "dp"),
        P(("sweep", "dp"), None),
        P("sweep", "dp"),
    )
    return jax.shard_map(
        per_device,
        mesh=mesh,
        in_specs=placed,
        out_specs=P(("sweep", "expert", "dp"), None),
        check_vma=False,
    )
```

profile of v0, /device:TPU:0, one launch (start us, length us, event | category | flops | bytes accessed | tf_op | source)
XLA Modules:
  0.0 332.9 jit_solution(2886106537347402265)
XLA Ops:
  6.5 0.0 copy-start
  6.5 0.0 all-gather.7.cloned.1.call-start
  6.5 0.7 all-gather.7.cloned.1.call-update
  7.3 0.0 copy-start.2
  7.3 0.0 copy-start.3
  7.3 0.0 all-gather.9.cloned.1.call-start
  7.3 0.7 all-gather.9.cloned.1.call-update
  8.0 0.0 all-gather.11.cloned.1.call-start
  8.1 1.1 convert_reduce_fusion.1
  9.2 1.2 fusion.20
  10.5 0.0 copy-done
  10.5 0.2 fusion.21
  10.8 12.7 %all_to_all.24 = bf16[128,4,384]{2,0,1:T(8,128)(2,1)} all-to-all(bf16[128,4,384]{2,0,1:T(8,128)(2,1)S(1)} %bitcast.37), channel_id=1, replica_groups=mesh['sweep'=2,'expert'=4,'dp'=4] {'dp'}, dimensions={1} | all-to-all | bytes 786432 | tf_op jit(solution)/shard_map/all_to_all | solution.py:132
  23.5 12.9 %all-gather.7.cloned.1.call-done = bf16[1536,768]{1,0:T(8,128)(2,1)} async-done(((bf16[384,768]{1,0:T(8,128)(2,1)}), bf16[1536,768]{1,0:T(8,128)(2,1)}) %all-gather.7.cloned.1.call-update) | async-done | bytes 2359312 | tf_op jit(solution)/shard_map/all_gather | solution.py:126
  36.4 26.3 %all-gather.9.cloned.1.call-done = bf16[768,1536]{1,0:T(8,128)(2,1)} async-done(((bf16[768,384]{1,0:T(8,128)(2,1)}), bf16[768,1536]{1,0:T(8,128)(2,1)}) %all-gather.9.cloned.1.call-update) | async-done | bytes 2359312 | tf_op jit(solution)/shard_map/all_gather | solution.py:127
  62.7 0.0 all-gather.11.cloned.1.call-update
  62.8 0.0 reduce-scatter.5.cloned.1.call-start
  62.8 0.0 copy-done.2
  62.8 0.0 copy-done.3
  62.9 21.5 %all-gather = f32[256,128]{1,0:T(8,128)S(1)} all-gather(f32[16,128]{1,0:T(8,128)S(1)} %maximum_bitcast_fusion), channel_id=2, replica_groups=mesh['sweep'=2,'expert'=4,'dp'=4] {'expert','dp'}, dimensions={0}, use_global_device_ids=true | all-gather | bytes 139264 | tf_op jit(solution)/shard_map/all_gather | solution.py:130
  84.4 0.2 compare_reduce_fusion
  84.6 0.2 fusion.16
  84.7 0.7 copy.14
  85.4 15.9 %all-gather.11.cloned.1.call-done.x_ref = bf16[2048,384]{1,0:T(8,128)(2,1)} async-done(((bf16[512,384]{1,0:T(8,128)(2,1)}), bf16[2048,384]{1,0:T(8,128)(2,1)}) %all-gather.11.cloned.1.call-update) | async-done | bytes 1572880 | tf_op jit(solution)/shard_map/all_gather | solution.py:136
  101.3 9.9 %shard_map.74 = bf16[4,8,1,80,768]{4,3,2,1,0:T(8,128)(2,1)} custom-call(bf16[2048,384]{1,0:T(8,128)(2,1)} %all-gather.11.cloned.1.call-done.x_ref, s32[16,1,2048]{2,1,0:T(1,128)} %bitcast.30, bf16[16,384,768]{2,1,0:T(8,128)(2,1)} %w_ref.5), custom_call_target="tpu_custom_call" | custom-call | flops 2516582400 | bytes 10223616 | tf_op jit(solution)/shard_map/pallas_call | solution.py:40
  111.2 0.0 reduce-scatter.5.cloned.1.call-update
  111.2 0.0 reduce-scatter.3.cloned.1.call-start
  111.3 10.1 %shard_map.73 = bf16[4,8,1,80,768]{4,3,2,1,0:T(8,128)(2,1)} custom-call(bf16[2048,384]{1,0:T(8,128)(2,1)} %all-gather.11.cloned.1.call-done.x_ref, s32[16,1,2048]{2,1,0:T(1,128)} %bitcast.31, bf16[16,384,768]{2,1,0:T(8,128)(2,1)} %w_ref.5), custom_call_target="tpu_custom_call" | custom-call | flops 2516582400 | bytes 10223616 | tf_op jit(solution)/shard_map/pallas_call | solution.py:40
  121.4 0.0 reduce-scatter.3.cloned.1.call-update
  121.4 0.0 all-gather.15.cloned.1.call-start
  121.4 32.1 %reduce-scatter.5.cloned.1.call-done = bf16[1,8,1,80,768]{4,3,2,1,0:T(8,128)(2,1)} async-done(((bf16[4,8,1,80,768]{4,3,2,1,0:T(8,128)(2,1)}), bf16[1,8,1,80,768]{4,3,2,1,0:T(8,128)(2,1)}) %reduce-scatter.5.cloned.1.call-update) | async-done | bytes 983056 | tf_op jit(solution)/shard_map/reduce_scatter | solution.py:161
  153.5 2.9 fusion.13
  156.5 0.0 all-gather.15.cloned.1.call-update
  156.5 0.0 all-gather.13.cloned.1.call-start
  156.5 42.3 %reduce-scatter.3.cloned.1.call-done = bf16[1,8,1,80,768]{4,3,2,1,0:T(8,128)(2,1)} async-done(((bf16[4,8,1,80,768]{4,3,2,1,0:T(8,128)(2,1)}), bf16[1,8,1,80,768]{4,3,2,1,0:T(8,128)(2,1)}) %reduce-scatter.3.cloned.1.call-update) | async-done | bytes 983056 | tf_op jit(solution)/shard_map/reduce_scatter | solution.py:161
  198.9 2.8 fusion.7
  201.7 0.0 all-gather.13.cloned.1.call-update
  201.7 0.2 fusion.17
  201.9 0.7 copy.15
  202.6 30.7 %all-gather.15.cloned.1.call-done.h_ref = bf16[4,8,1,80,768]{4,3,2,1,0:T(8,128)(2,1)} async-done(((bf16[1,8,1,80,768]{4,3,2,1,0:T(8,128)(2,1)}), bf16[4,8,1,80,768]{4,3,2,1,0:T(8,128)(2,1)}) %all-gather.15.cloned.1.call-update) | async-done | bytes 3932176 | tf_op jit(solution)/shard_map/all_gather | solution.py:166
  233.3 12.1 %shard_map.75.refs_0_ = f32[2048,384]{1,0:T(8,128)} custom-call(bf16[4,8,1,80,768]{4,3,2,1,0:T(8,128)(2,1)} %all-gather.15.cloned.1.call-done.h_ref, s32[16,1,2048]{2,1,0:T(1,128)} %bitcast.32, f32[16,1,2048]{2,1,0:T(1,128)} %bitcast.39, bf16[16,768,384]{2,1,0:T(8,128)(2,1)} %w_ref.7), custom_call_target="tpu_custom_call" | custom-call | flops 4529848320 | bytes 11796480 | tf_op jit(solution)/shard_map/pallas_call | solution.py:94
  245.4 22.5 %all-gather.13.cloned.1.call-done.h_ref = bf16[4,8,1,80,768]{4,3,2,1,0:T(8,128)(2,1)} async-done(((bf16[1,8,1,80,768]{4,3,2,1,0:T(8,128)(2,1)}), bf16[4,8,1,80,768]{4,3,2,1,0:T(8,128)(2,1)}) %all-gather.13.cloned.1.call-update) | async-done | bytes 3932176 | tf_op jit(solution)/shard_map/all_gather | solution.py:166
  267.9 12.4 %shard_map.76 = bf16[2048,384]{1,0:T(8,128)(2,1)} custom-call(bf16[4,8,1,80,768]{4,3,2,1,0:T(8,128)(2,1)} %all-gather.13.cloned.1.call-done.h_ref, s32[16,1,2048]{2,1,0:T(1,128)} %bitcast.33, f32[16,1,2048]{2,1,0:T(1,128)} %bitcast.40, bf16[16,768,384]{2,1,0:T(8,128)(2,1)} %w_ref.7, f32[2048,384]{1,0:T(8,128)} %shard_map.75.refs_0_), custom_call_target="tpu_custom_call" | custom-call | flops 4529848320 | bytes 11796480 | tf_op jit(solution)/shard_map/pallas_call | solution.py:94
  280.3 40.6 %all_to_all.25 = bf16[16,128,384]{2,1,0:T(8,128)(2,1)S(1)} all-to-all(bf16[16,128,384]{2,1,0:T(8,128)(2,1)} %bitcast.28), channel_id=1, replica_groups=mesh['sweep'=2,'expert'=4,'dp'=4] {'expert','dp'}, dimensions={0} | all-to-all | bytes 3145728 | tf_op jit(solution)/shard_map/all_to_all | solution.py:179
  320.9 0.2 convert_reduce_fusion
  321.1 0.1 copy.18
  321.2 1.3 copy-done.1
  322.5 3.5 %fusion.1 = bf16[128,1536]{1,0:T(8,128)(2,1)} fusion(f32[128,1536]{1,0:T(8,128)S(1)} %bitcast.35, bf16[768,1536]{1,0:T(8,128)(2,1)} %all-gather.9.cloned.1.call-done, bf16[128,1536]{1,0:T(8,128)(2,1)S(1)} %copy-done, bf16[1536,768]{1,0:T(8,128)(2,1)S(1)} %copy-done.1, f32[128]{0:T(128)S(1)} %add_rsqrt_fusion, f32[128]{0:T(128)S(1)} %broadcast_multiply_fusion), kind=kOutput, calls=%fused_computation.11 | convolution fusion | flops 606437376 | bytes 6292480 | tf_op jit(solution)/shard_map/dot_general | solution.py:170
  (9 shorter events, 0.1 us)
Async XLA Ops:
  6.5 3.9 %copy-start = (bf16[128,1536]{1,0:T(8,128)(2,1)S(1)}, bf16[128,1536]{1,0:T(8,128)(2,1)}, u32[]{:S(2)}) copy-start(bf16[128,1536]{1,0:T(8,128)(2,1)} %param.7) | copy-start | bytes 1179652
  6.5 29.9 %all-gather.7.cloned.1.call-start = ((), (), s32[]{:S(2)}) async-start(), calls=%async_computation.4 | async-start | bytes 2949120 | tf_op jit(solution)/shard_map/all_gather | solution.py:126
  7.3 55.6 %copy-start.2 = (s32[128,8]{0,1:T(8,128)S(1)}, s32[128,8]{0,1:T(8,128)}, u32[]{:S(2)}) copy-start(s32[128,8]{0,1:T(8,128)} %param.8) | copy-start | bytes 12292
  7.3 55.6 %copy-start.3 = (f32[128,8]{0,1:T(8,128)S(1)}, f32[128,8]{0,1:T(8,128)}, u32[]{:S(2)}) copy-start(f32[128,8]{0,1:T(8,128)} %param.9) | copy-start | bytes 12292
  7.3 55.5 %all-gather.9.cloned.1.call-start = ((), (), s32[]{:S(2)}) async-start(), calls=%async_computation.5 | async-start | bytes 2949120 | tf_op jit(solution)/shard_map/all_gather | solution.py:127
  8.0 93.3 %all-gather.11.cloned.1.call-start = ((), (), s32[]{:S(2)}) async-start(), calls=%async_computation.6 | async-start | bytes 1966080 | tf_op jit(solution)/shard_map/all_gather | solution.py:136
  62.8 90.8 %reduce-scatter.5.cloned.1.call-start = ((), (), s32[]{:S(2)}) async-start(), calls=%async_computation.9 | async-start | bytes 4915200 | tf_op jit(solution)/shard_map/reduce_scatter | solution.py:161
  111.2 87.6 %reduce-scatter.3.cloned.1.call-start = ((), (), s32[]{:S(2)}) async-start(), calls=%async_computation.7 | async-start | bytes 4915200 | tf_op jit(solution)/shard_map/reduce_scatter | solution.py:161
  121.4 111.9 %all-gather.15.cloned.1.call-start = ((), (), s32[]{:S(2)}) async-start(), calls=%async_computation.10 | async-start | bytes 4915200 | tf_op jit(solution)/shard_map/all_gather | solution.py:166
  156.5 111.4 %all-gather.13.cloned.1.call-start = ((), (), s32[]{:S(2)}) async-start(), calls=%async_computation.8 | async-start | bytes 4915200 | tf_op jit(solution)/shard_map/all_gather | solution.py:166
  320.9 1.7 copy-start.1
Sparse Core Ops, SparseCore 0:
  8.9 27.4 all-gather.6
  38.0 24.7 all-gather.8
  64.3 36.9 all-gather.10
  111.3 42.1 reduce-scatter.4
  155.9 42.9 reduce-scatter.2
  200.3 32.9 all-gather.14
  234.8 32.9 all-gather.12
where the time goes:
time: 335 us; the launch traced here: 333 us
  waiting for transfers between devices  184 us (55%)
  blocking collectives  74.8 us (22%)
  Pallas kernels  44.5 us (13%)
  between operations  13.6 us (4%)
  other arithmetic  9.05 us (3%)
  matrix products  3.69 us (1%)
    reduce_scatter x2, waiting for transfers between devices, per_device(): parts.append(lax.psum_scatter(pre, 'dp', scatter_dimension=0, tiled=True))  74.4 us
    all_gather x2, waiting for transfers between devices, per_device(): hidden.append(lax.all_gather(act, 'dp', axis=0, tiled=True))  53.1 us
    all_to_all x1, blocking collectives, per_device(): lax.all_to_all(routed.reshape(block_count, row_count, width), ('expert',...  40.6 us
    all_gather x1, waiting for transfers between devices, per_device(): full_shared_out = lax.all_gather(shared_out, 'dp', axis=1, tiled=True)  26.3 us
    pallas_call x2, Pallas kernels, second_projection(): pl.pallas_call(functools.partial(second_kernel, runs, run_tokens), grid=(...  24.5 us
    all_gather x1, blocking collectives, per_device(): named = lax.all_gather(named, ('expert', 'dp'), axis=0, tiled=False)  21.5 us
    pallas_call x2, Pallas kernels, first_projection(): pl.pallas_call(functools.partial(first_kernel, runs, run_tokens), grid=(c...  20 us
    all_gather x1, waiting for transfers between devices, per_device(): x = lax.all_gather(columns, 'expert', axis=0, tiled=True)  15.9 us
  transfers between devices with their start and end apart: 7, of which 7 were waited for; matrix products, arithmetic and copies ran while one was open for 3% of the time, Pallas kernels for 7%

commit v1 on v0

--- a/solution.py
+++ b/solution.py
@@ -188,6 +188,496 @@
     return (tokens.astype(jnp.float32) + shared_result + own).astype(jnp.bfloat16)
 
 
+def start_of(index, size):
+    return pl.ds(pl.multiple_of(index * size, size), size)
+
+
+def fused_kernel(
+    sizes,
+    tok_ref,
+    named_ref,
+    win_hbm,
+    wout_hbm,
+    sin_hbm,
+    sout_hbm,
+    out_ref,
+    norm,
+    xall,
+    meta,
+    win,
+    wout,
+    sin,
+    sout,
+    keys,
+    gates,
+    pick,
+    gslot,
+    rows,
+    send,
+    recv,
+    ssend,
+    srecv,
+    shared,
+    scaled,
+    own,
+    psend,
+    precv,
+    zsend,
+    zrecv,
+    fsend,
+    frecv,
+    lsem,
+    wssem,
+    wrsem,
+    xsem,
+    zssem,
+    zrsem,
+    rssem,
+    rrsem,
+    mssem,
+    mrsem,
+    pssem,
+    prsem,
+    ssem,
+    srsem,
+    dssem,
+    drsem,
+    ossem,
+    orsem,
+):
+    planes, chips, cores = sizes
+    dp = chips * cores
+    n = planes * dp
+    tok_rows, width = tok_ref.shape
+    picks = named_ref.shape[0] // 2
+    half = width // chips
+    part = half // cores
+    experts = win.shape[0]
+    local = experts * cores
+    slots = pick.shape[2]
+    span = pick.shape[3]
+    own_rows = chips * tok_rows
+
+    z = lax.axis_index("expert")
+    d = lax.axis_index("dp")
+    c = d % cores
+    x = d // cores
+    oc = 1 - c
+    ox = 1 - x
+    partner = {"dp": x * cores + oc}
+    across = {"dp": ox * cores + c}
+    s = c * chips + x
+
+    def remote(src, dst, s_sem, r_sem, device):
+        return pltpu.make_async_remote_copy(
+            src_ref=src,
+            dst_ref=dst,
+            send_sem=s_sem,
+            recv_sem=r_sem,
+            device_id=device,
+            device_id_type=pl.DeviceIdType.MESH,
+        )
+
+    def loop(first, last, body):
+        def step(i, carry):
+            body(i)
+            return carry
+
+        lax.fori_loop(first, last, step, 0)
+
+    def place(r):
+        spot = lax.rem(z * dp + d + r, n)
+        return {"expert": spot // dp, "dp": lax.rem(spot, dp)}
+
+    def local_in(e):
+        return pltpu.make_async_copy(
+            win_hbm.at[c * experts + e], win.at[e, start_of(c, part)], lsem.at[e]
+        )
+
+    def local_out(e):
+        return pltpu.make_async_copy(
+            wout_hbm.at[c * experts + e],
+            wout.at[e, :, start_of(c, part)],
+            lsem.at[experts + e],
+        )
+
+    def local_shared_in():
+        return pltpu.make_async_copy(sin_hbm, sin.at[start_of(c, part)], lsem.at[2 * experts])
+
+    def local_shared_out():
+        return pltpu.make_async_copy(
+            sout_hbm, sout.at[:, start_of(c, part)], lsem.at[2 * experts + 1]
+        )
+
+    def partner_in(e):
+        return remote(
+            win_hbm.at[oc * experts + e],
+            win.at[e, start_of(c, part)],
+            wssem.at[e],
+            wrsem.at[e],
+            partner,
+        )
+
+    def partner_out(e):
+        return remote(
+            wout_hbm.at[oc * experts + e],
+            wout.at[e, :, start_of(c, part)],
+            wssem.at[experts + e],
+            wrsem.at[experts + e],
+            partner,
+        )
+
+    def partner_shared_in():
+        return remote(
+            sin_hbm,
+            sin.at[start_of(c, part)],
+            wssem.at[2 * experts],
+            wrsem.at[2 * experts],
+            partner,
+        )
+
+    def partner_shared_out():
+        return remote(
+            sout_hbm,
+            sout.at[:, start_of(c, part)],
+            wssem.at[2 * experts + 1],
+            wrsem.at[2 * experts + 1],
+            partner,
+        )
+
+    def token_swap():
+        return remote(
+            norm.at[:, start_of(ox, half)], xall.at[z, c, x], xsem.at[0], xsem.at[1], across
+        )
+
+    def to_plane(i, b):
+        return remote(
+            xall.at[z, c, b],
+            xall.at[z, c, b],
+            zssem.at[i - 1, b],
+            zrsem.at[i - 1, b],
+            {"expert": lax.rem(z - i + planes, planes)},
+        )
+
+    def relay(i, b):
+        p = lax.rem(z + i, planes)
+        return remote(
+            xall.at[p, c, b], xall.at[p, c, b], rssem.at[i, b], rrsem.at[i, b], partner
+        )
+
+    def tell(r):
+        return remote(named_ref, meta.at[z, s], mssem.at[r], mrsem.at[r], place(r))
+
+    def swap(k, e):
+        return remote(send.at[k, e], recv.at[k, e], pssem.at[k, e], prsem.at[k, e], across)
+
+    def shared_swap(b):
+        return remote(ssend.at[b], srecv.at[b], ssem.at[b], srsem.at[b], across)
+
+    def pair(k):
+        return remote(psend.at[k], precv.at[k], dssem.at[k], drsem.at[k], partner)
+
+    def give(k):
+        return remote(
+            zsend.at[k],
+            zrecv.at[k],
+            ossem.at[k],
+            orsem.at[k],
+            {"expert": lax.rem(z + k + 1, planes)},
+        )
+
+    def finish():
+        return remote(fsend, frecv, xsem.at[2], xsem.at[3], across)
+
+    barrier = pltpu.get_barrier_semaphore()
+    loop(
+        1,
+        n,
+        lambda r: pl.semaphore_signal(
+            barrier, inc=1, device_id=place(r), device_id_type=pl.DeviceIdType.MESH
+        ),
+    )
+    local_shared_in().start()
+    loop(0, experts, lambda e: local_in(e).start())
+    local_shared_out().start()
+    loop(0, experts, lambda e: local_out(e).start())
+
+    values = tok_ref[...].astype(jnp.float32)
+    center = values - jnp.mean(values, axis=-1, keepdims=True)
+    spread = jnp.mean(center * center, axis=-1, keepdims=True)
+    norm[...] = (center * lax.rsqrt(spread + 1e-06)).astype(jnp.bfloat16)
+    xall[z, c, x] = norm[:, start_of(x, half)]
+    meta[z, s] = named_ref[...]
+
+    pl.semaphore_wait(barrier, n - 1)
+    token_swap().start()
+    relay(0, x).start()
+    loop(1, planes, lambda i: to_plane(i, x).start())
+    partner_shared_in().start()
+    loop(1, n, lambda r: tell(r).start())
+    loop(0, experts, lambda e: partner_in(e).start())
+    partner_shared_out().start()
+    loop(0, experts, lambda e: partner_out(e).start())
+
+    def shared_first(b):
+        pre = jnp.dot(xall[z, c, b], sin[...], preferred_element_type=jnp.float32)
+        ssend[b] = pre.astype(jnp.bfloat16)
+        shared_swap(b).start()
+
+    local_shared_in().wait()
+    partner_shared_in().wait_recv()
+    shared_first(x)
+    token_swap().wait_recv()
+    relay(0, ox).start()
+    loop(1, planes, lambda i: to_plane(i, ox).start())
+    shared_first(ox)
+    loop(1, n, lambda r: tell(r).wait_recv())
+
+    before = jnp.where(
+        lax.broadcasted_iota(jnp.int32, (tok_rows, tok_rows), 0)
+        < lax.broadcasted_iota(jnp.int32, (tok_rows, tok_rows), 1),
+        1.0,
+        0.0,
+    ).astype(jnp.bfloat16)
+
+    def first_stage(k, weights_wait):
+        i = lax.rem(k + 1, planes)
+        p = lax.rem(z + i, planes)
+        turn = lax.rem(k, 2)
+
+        ids = jnp.concatenate([meta[p, b, :picks] for b in range(dp)], axis=1)
+        weights = jnp.concatenate([meta[p, b, picks:] for b in range(dp)], axis=1)
+        chosen, gate = [], []
+        for e in range(experts):
+            match = ids == (z * local + c * experts + e).astype(jnp.float32)
+            chosen.append(jnp.max(jnp.where(match, 1.0, 0.0), axis=0, keepdims=True))
+            gate.append(jnp.sum(jnp.where(match, weights, 0.0), axis=0, keepdims=True))
+        chosen = jnp.concatenate(chosen, axis=0)
+        gates[...] = jnp.concatenate(gate, axis=0)
+        for b in range(dp):
+            lanes = slice(b * tok_rows, (b + 1) * tok_rows)
+            mine = chosen[:, lanes]
+            earlier = jnp.dot(
+                mine.astype(jnp.bfloat16), before, preferred_element_type=jnp.float32
+            )
+            keys[:, lanes] = jnp.where(mine > 0.5, earlier + float(b * CAP), -1.0).astype(
+                jnp.int32
+            )
+
+        def choose(e):
+            row = lax.broadcasted_iota(jnp.int32, (slots, span), 0)
+            match = row == keys[pl.ds(e, 1), :]
+            pick[turn, e] = jnp.where(match, 1.0, 0.0).astype(jnp.bfloat16)
+            gate = jnp.sum(
+                jnp.where(match, gates[pl.ds(e, 1), :], 0.0), axis=1, keepdims=True
+            )
+            gslot[turn, e] = jnp.broadcast_to(gate, gslot.shape[2:])
+
+        loop(0, experts, choose)
+
+        @pl.when(i > 0)
+        def _():
+            for b in range(chips):
+                to_plane(lax.max(i, 1), b).wait_recv()
+                relay(i, b).start()
+
+        for b in range(chips):
+            relay(i, b).wait_recv()
+        plane = xall[p].reshape(span, half)
+        chosen_rows = jnp.dot(
+            pick[turn].reshape(experts * slots, span), plane, preferred_element_type=jnp.float32
+        )
+        rows[...] = chosen_rows.astype(jnp.bfloat16).reshape(rows.shape)
+
+        def project(e):
+            if weights_wait:
+                local_in(e).wait()
+                partner_in(e).wait_recv()
+            pre = jnp.dot(rows[e], win[e], preferred_element_type=jnp.float32)
+            send[k, e] = pre.astype(jnp.bfloat16)
+            swap(k, e).start()
+
+        loop(0, experts, project)
+
+    def second_stage(k):
+        turn = lax.rem(k, 2)
+
+        def project(e):
+            swap(k, e).wait_recv()
+            total = send[k, e].astype(jnp.float32) + recv[k, e].astype(jnp.float32)
+            h = jax.nn.gelu(total).astype(jnp.bfloat16)
+            result = jnp.dot(h, wout[e], preferred_element_type=jnp.float32)
+            scaled[e] = (result * gslot[turn, e][:, :1]).astype(jnp.bfloat16)
+
+        loop(0, experts, project)
+
+        def combine(core):
+            lanes = start_of(core, own_rows)
+            return lax.dot_general(
+                pick[turn, :, :, lanes].reshape(experts * slots, own_rows),
+                scaled[...].reshape(experts * slots, half),
+                (((0,), (0,)), ((), ())),
+                preferred_element_type=jnp.float32,
+            )
+
+        psend[k] = combine(oc).astype(jnp.bfloat16)
+        pair(k).start()
+        own[...] = combine(c)
+        pair(k).wait_recv()
+        own[...] += precv[k].astype(jnp.float32)
+
+    def shared_second():
+        local_shared_out().wait()
+        partner_shared_out().wait_recv()
+        for b in range(chips):
+            shared_swap(b).wait_recv()
+        total = ssend[...].astype(jnp.float32) + srecv[...].astype(jnp.float32)
+        h = jax.nn.gelu(total).astype(jnp.bfloat16).reshape(own_rows, -1)
+        shared[...] = jnp.dot(h, sout[...], preferred_element_type=jnp.float32)
+
+    first_stage(0, True)
+    shared_second()
+    for e in range(experts):
+        local_out(e).wait()
+        partner_out(e).wait_recv()
+
+    def plane_step(k):
+        first_stage(k + 1, False)
+        second_stage(k)
+        zsend[k] = own[...].astype(jnp.bfloat16)
+        give(k).start()
+
+    loop(0, planes - 1, plane_step)
+    second_stage(planes - 1)
+    total = own[...] + shared[...]
+    for k in range(planes - 1):
+        give(k).wait_recv()
+        total = total + zrecv[k].astype(jnp.float32)
+    own[...] = total
+    fsend[...] = own[start_of(ox, tok_rows), :].astype(jnp.bfloat16)
+    finish().start()
+    mine = start_of(x, half)
+    theirs = start_of(ox, half)
+    out_ref[:, mine] = (
+        tok_ref[:, mine].astype(jnp.float32) + own[start_of(x, tok_rows), :]
+    ).astype(out_ref.dtype)
+    finish().wait_recv()
+    out_ref[:, theirs] = (
+        tok_ref[:, theirs].astype(jnp.float32) + frecv[...].astype(jnp.float32)
+    ).astype(out_ref.dtype)
+
+    token_swap().wait_send()
+    partner_shared_in().wait_send()
+    partner_shared_out().wait_send()
+    finish().wait_send()
+    loop(1, n, lambda r: tell(r).wait_send())
+
+    def weights_sent(e):
+        partner_in(e).wait_send()
+        partner_out(e).wait_send()
+
+    loop(0, experts, weights_sent)
+    for b in range(chips):
+        shared_swap(b).wait_send()
+
+        def sent(i):
+            relay(i, b).wait_send()
+
+        loop(0, planes, sent)
+        loop(1, planes, lambda i: to_plane(i, b).wait_send())
+
+    def plane_sent(k):
+        loop(0, experts, lambda e: swap(k, e).wait_send())
+        pair(k).wait_send()
+
+    loop(0, planes, plane_sent)
+    loop(0, planes - 1, lambda k: give(k).wait_send())
+
+
+def fused(tokens, expert_ids, gate_weights, expert_in, expert_out, shared_in, shared_out):
+    tok_rows, width = tokens.shape
+    picks = expert_ids.shape[1]
+    planes, dp = lax.axis_size("expert"), lax.axis_size("dp")
+    cores, chips = 2, dp // 2
+    local, part, hidden = expert_in.shape
+    experts = local // cores
+    half = width // chips
+    slots, span = dp * CAP, dp * tok_rows
+    own_rows = chips * tok_rows
+    named = jnp.concatenate([expert_ids.astype(jnp.float32), gate_weights], axis=1).T
+    bf16, f32 = jnp.bfloat16, jnp.float32
+    vmem, dma = pltpu.VMEM, pltpu.SemaphoreType.DMA
+    scratch = [
+        vmem((tok_rows, width), bf16),
+        vmem((planes, cores, chips, tok_rows, half), bf16),
+        vmem((planes, dp, 2 * picks, tok_rows), f32),
+        vmem((experts, half, hidden), bf16),
+        vmem((experts, hidden, half), bf16),
+        vmem((half, hidden), bf16),
+        vmem((hidden, half), bf16),
+        vmem((experts, span), jnp.int32),
+        vmem((experts, span), f32),
+        vmem((2, experts, slots, span), bf16),
+        vmem((2, experts, slots, 128), f32),
+        vmem((experts, slots, half), bf16),
+        vmem((planes, experts, slots, hidden), bf16),
+        vmem((planes, experts, slots, hidden), bf16),
+        vmem((chips, tok_rows, hidden), bf16),
+        vmem((chips, tok_rows, hidden), bf16),
+        vmem((own_rows, half), f32),
+        vmem((experts, slots, half), bf16),
+        vmem((own_rows, half), f32),
+        vmem((planes, own_rows, half), bf16),
+        vmem((planes, own_rows, half), bf16),
+        vmem((planes - 1, own_rows, half), bf16),
+        vmem((planes - 1, own_rows, half), bf16),
+        vmem((tok_rows, half), bf16),
+        vmem((tok_rows, half), bf16),
+        dma((2 * experts + 2,)),
+        dma((2 * experts + 2,)),
+        dma((2 * experts + 2,)),
+        dma((4,)),
+        dma((planes - 1, chips)),
+        dma((planes - 1, chips)),
+        dma((planes, chips)),
+        dma((planes, chips)),
+        dma((planes * dp,)),
+        dma((planes * dp,)),
+        dma((planes, experts)),
+        dma((planes, experts)),
+        dma((chips,)),
+        dma((chips,)),
+        dma((planes,)),
+        dma((planes,)),
+        dma((planes - 1,)),
+        dma((planes - 1,)),
+    ]
+    whole = pl.BlockSpec(memory_space=pltpu.VMEM)
+    apart = pl.BlockSpec(memory_space=pl.ANY)
+    return pl.pallas_call(
+        functools.partial(fused_kernel, (planes, chips, cores)),
+        in_specs=[whole, whole, apart, apart, apart, apart],
+        out_specs=whole,
+        out_shape=jax.ShapeDtypeStruct((tok_rows, width), tokens.dtype),
+        scratch_shapes=scratch,
+        compiler_params=pltpu.CompilerParams(
+            collective_id=0, has_side_effects=True, vmem_limit_bytes=63 * 1024 * 1024
+        ),
+    )(tokens, named, expert_in, expert_out, shared_in, shared_out)
+
+
+def fits(mesh, args):
+    planes, dp = mesh.shape["expert"], mesh.shape["dp"]
+    tokens, expert_in = args[0], args[3]
+    return (
+        dp == 4
+        and 1 < planes <= 8
+        and expert_in.shape[0] // (mesh.shape["sweep"] * planes) % 2 == 0
+        and expert_in.shape[0] // (mesh.shape["sweep"] * planes) <= 16
+        and tokens.shape[0] // (mesh.shape["sweep"] * planes * dp) == 128
+    )
+
+
 def solution(mesh):
     placed = (
         P(("sweep", "expert", "dp"), None),
@@ -198,10 +688,14 @@
         P(("sweep", "dp"), None),
         P("sweep", "dp"),
     )
-    return jax.shard_map(
-        per_device,
-        mesh=mesh,
-        in_specs=placed,
-        out_specs=P(("sweep", "expert", "dp"), None),
-        check_vma=False,
-    )
+
+    def run(*args):
+        return jax.shard_map(
+            fused if fits(mesh, args) else per_device,
+            mesh=mesh,
+            in_specs=placed,
+            out_specs=P(("sweep", "expert", "dp"), None),
+            check_vma=False,
+        )(*args)
+
+    return run

time: 335 us -> 142 us (0.42)
  waiting for transfers between devices: 184 us -> 0 us
  Pallas kernels: 44.5 us -> 138 us
  blocking collectives: 74.8 us -> 0 us
  between operations: 13.6 us -> 0.01 us
  other arithmetic: 9.05 us -> 1.97 us
  matrix products: 3.69 us -> 0 us
    all_gather x5 -> x0, waiting for transfers between devices: 108 us -> none  [the longest x2 53.1 us: per_device(): hidden.append(lax.all_gather(act, 'dp', axis=0, tiled=True))]
    pallas_call x4 -> x1, Pallas kernels: 44.5 us -> 138 us  [fused(): pl.pallas_call(functools.partial(fused_kernel, (planes, chips, cores)), i...]
    reduce_scatter x2 -> x0, waiting for transfers between devices: 74.4 us -> none  [per_device(): parts.append(lax.psum_scatter(pre, 'dp', scatter_dimension=0, tiled=True))]
    all_to_all x2 -> x0, blocking collectives: 53.4 us -> none  [the longest x1 40.6 us: per_device(): lax.all_to_all(routed.reshape(block_count, row_count, width), ('expert',...]
    all_gather x1 -> x0, blocking collectives: 21.5 us -> none  [per_device(): named = lax.all_gather(named, ('expert', 'dp'), axis=0, tiled=False)]
    convert_element_type x5 -> x1, other arithmetic: 6.02 us -> 0.69 us  [fused(): expert_ids.astype(jnp.float32)]
    dot_general x2 -> x0, matrix products: 3.69 us -> none  [the longest x1 3.52 us: per_device(): jnp.dot(shared_hidden, full_shared_out, preferred_element_type=jnp.float32)]
  transfers between devices with their start and end apart: 7 -> 0, of which waited for: 7 -> 0; matrix products, arithmetic and copies ran while one was open for 3% -> 0% of each run, Pallas kernels for 7% -> 0%
where the time goes in v1:
time: 142 us; the launch traced here: 141 us
  Pallas kernels  138 us (97%)
  other arithmetic  1.97 us (1%)
  local copies, waits for them, and re-layouts  1.77 us (1%)
    pallas_call x1, Pallas kernels, fused(): pl.pallas_call(functools.partial(fused_kernel, (planes, chips, cores)), i...  138 us

profile of v1, /device:TPU:0, one launch (start us, length us, event | category | flops | bytes accessed | tf_op | source)
XLA Modules:
  0.0 141.3 jit_solution(14976896464745169731)
XLA Ops:
  0.0 0.7 convert_element_type.3
  0.7 1.3 maximum_bitcast_fusion.named_ref
  2.0 137.6 %shard_map.73 = bf16[128,1536]{1,0:T(8,128)(2,1)} custom-call(bf16[128,1536]{1,0:T(8,128)(2,1)} %tok_ref.1, f32[16,128]{1,0:T(8,128)} %maximum_bitcast_fusion.named_ref, bf16[16,384,768]{2,1,0:T(8,128)(2,1)} %win_hbm.1, bf16[16,768,384]{2,1,0:T(8,128)(2,1)} %wout_hbm.1, bf16[384,768]{1,0:T(8,128)(2,1)} %sin_hbm.1, bf16[768,384]{1,0:T(8,128)(2,1)} %sout_hbm.1), custom_call_target="tpu_custom_call" | custom-call | tf_op jit(solution)/shard_map/pallas_call | solution.py:657
  139.5 1.8 %copy.9 = bf16[128,1536]{1,0:T(8,128)(2,1)} copy(bf16[128,1536]{1,0:T(8,128)(2,1)} %shard_map.73) | data formatting | bytes 786432

commit v2 on v1

--- a/solution.py
+++ b/solution.py
@@ -192,15 +192,22 @@
     return pl.ds(pl.multiple_of(index * size, size), size)
 
 
+HEAD = 4
+
+
 def fused_kernel(
     sizes,
-    tok_ref,
-    named_ref,
+    tok_hbm,
+    ids_hbm,
+    gate_hbm,
     win_hbm,
     wout_hbm,
     sin_hbm,
     sout_hbm,
     out_ref,
+    tok,
+    ids_in,
+    gate_in,
     norm,
     xall,
     meta,
@@ -220,43 +227,50 @@
     shared,
     scaled,
     own,
+    other,
     psend,
     precv,
+    osend,
+    orecv,
     zsend,
     zrecv,
     fsend,
     frecv,
+    isem,
     lsem,
     wssem,
     wrsem,
-    xsem,
+    xssem,
+    xrsem,
     zssem,
     zrsem,
     rssem,
     rrsem,
-    mssem,
-    mrsem,
     pssem,
     prsem,
     ssem,
     srsem,
     dssem,
     drsem,
+    bssem,
+    brsem,
     ossem,
     orsem,
+    fssem,
+    frsem,
 ):
     planes, chips, cores = sizes
     dp = chips * cores
-    n = planes * dp
-    tok_rows, width = tok_ref.shape
-    picks = named_ref.shape[0] // 2
+    tok_rows, width = tok.shape
+    picks = ids_in.shape[0]
     half = width // chips
     part = half // cores
     experts = win.shape[0]
     local = experts * cores
-    slots = pick.shape[2]
-    span = pick.shape[3]
+    slots, span = pick.shape[2:]
     own_rows = chips * tok_rows
+    last = planes - 1
+    head = min(HEAD, experts)
 
     z = lax.axis_index("expert")
     d = lax.axis_index("dp")
@@ -266,7 +280,7 @@
     ox = 1 - x
     partner = {"dp": x * cores + oc}
     across = {"dp": ox * cores + c}
-    s = c * chips + x
+    mesh_ids = pl.DeviceIdType.MESH
 
     def remote(src, dst, s_sem, r_sem, device):
         return pltpu.make_async_remote_copy(
@@ -275,19 +289,18 @@
             send_sem=s_sem,
             recv_sem=r_sem,
             device_id=device,
-            device_id_type=pl.DeviceIdType.MESH,
-        )
-
-    def loop(first, last, body):
+            device_id_type=mesh_ids,
+        )
+
+    def loop(first, end, body):
         def step(i, carry):
             body(i)
             return carry
 
-        lax.fori_loop(first, last, step, 0)
-
-    def place(r):
-        spot = lax.rem(z * dp + d + r, n)
-        return {"expert": spot // dp, "dp": lax.rem(spot, dp)}
+        lax.fori_loop(first, end, step, 0)
+
+    def plane_at(i):
+        return {"expert": lax.rem(z + i, planes)}
 
     def local_in(e):
         return pltpu.make_async_copy(
@@ -345,28 +358,22 @@
             partner,
         )
 
-    def token_swap():
+    def block(p, b, kind):
+        return meta.at[p, c * chips + b] if kind else xall.at[p, c, b]
+
+    def token_swap(kind):
+        src = meta.at[z, c * chips + x] if kind else norm.at[:, start_of(ox, half)]
+        return remote(src, block(z, x, kind), xssem.at[kind], xrsem.at[kind], across)
+
+    def to_plane(i, b, kind):
+        ref = block(z, b, kind)
         return remote(
-            norm.at[:, start_of(ox, half)], xall.at[z, c, x], xsem.at[0], xsem.at[1], across
-        )
-
-    def to_plane(i, b):
-        return remote(
-            xall.at[z, c, b],
-            xall.at[z, c, b],
-            zssem.at[i - 1, b],
-            zrsem.at[i - 1, b],
-            {"expert": lax.rem(z - i + planes, planes)},
-        )
-
-    def relay(i, b):
-        p = lax.rem(z + i, planes)
-        return remote(
-            xall.at[p, c, b], xall.at[p, c, b], rssem.at[i, b], rrsem.at[i, b], partner
-        )
-
-    def tell(r):
-        return remote(named_ref, meta.at[z, s], mssem.at[r], mrsem.at[r], place(r))
+            ref, ref, zssem.at[i - 1, b, kind], zrsem.at[i - 1, b, kind], plane_at(planes - i)
+        )
+
+    def relay(i, b, kind):
+        ref = block(lax.rem(z + i, planes), b, kind)
+        return remote(ref, ref, rssem.at[i, b, kind], rrsem.at[i, b, kind], partner)
 
     def swap(k, e):
         return remote(send.at[k, e], recv.at[k, e], pssem.at[k, e], prsem.at[k, e], across)
@@ -377,47 +384,49 @@
     def pair(k):
         return remote(psend.at[k], precv.at[k], dssem.at[k], drsem.at[k], partner)
 
+    def own_pair(b):
+        return remote(osend.at[b], orecv.at[b], bssem.at[b], brsem.at[b], partner)
+
     def give(k):
-        return remote(
-            zsend.at[k],
-            zrecv.at[k],
-            ossem.at[k],
-            orsem.at[k],
-            {"expert": lax.rem(z + k + 1, planes)},
-        )
+        return remote(zsend.at[k], zrecv.at[k], ossem.at[k], orsem.at[k], plane_at(k + 1))
 
     def finish():
-        return remote(fsend, frecv, xsem.at[2], xsem.at[3], across)
+        return remote(fsend, frecv, fssem.at[0], frsem.at[0], across)
 
     barrier = pltpu.get_barrier_semaphore()
-    loop(
-        1,
-        n,
-        lambda r: pl.semaphore_signal(
-            barrier, inc=1, device_id=place(r), device_id_type=pl.DeviceIdType.MESH
-        ),
-    )
+    for device in [across, partner] + [plane_at(i) for i in range(1, planes)]:
+        pl.semaphore_signal(barrier, inc=1, device_id=device, device_id_type=mesh_ids)
+    read_tok = pltpu.make_async_copy(tok_hbm, tok, isem.at[0])
+    read_ids = pltpu.make_async_copy(ids_hbm, ids_in, isem.at[1])
+    read_gate = pltpu.make_async_copy(gate_hbm, gate_in, isem.at[2])
+    read_tok.start()
+    read_ids.start()
+    read_gate.start()
     local_shared_in().start()
     loop(0, experts, lambda e: local_in(e).start())
     local_shared_out().start()
     loop(0, experts, lambda e: local_out(e).start())
-
-    values = tok_ref[...].astype(jnp.float32)
+    read_ids.wait()
+    read_gate.wait()
+    meta[z, c * chips + x, :picks] = ids_in[...].astype(jnp.float32)
+    meta[z, c * chips + x, picks:] = gate_in[...]
+    read_tok.wait()
+    values = tok[...].astype(jnp.float32)
     center = values - jnp.mean(values, axis=-1, keepdims=True)
     spread = jnp.mean(center * center, axis=-1, keepdims=True)
     norm[...] = (center * lax.rsqrt(spread + 1e-06)).astype(jnp.bfloat16)
     xall[z, c, x] = norm[:, start_of(x, half)]
-    meta[z, s] = named_ref[...]
-
-    pl.semaphore_wait(barrier, n - 1)
-    token_swap().start()
-    relay(0, x).start()
-    loop(1, planes, lambda i: to_plane(i, x).start())
+
+    pl.semaphore_wait(barrier, planes + 1)
+    early = min(3, experts)
+    for kind in (1, 0):
+        token_swap(kind).start()
+    for kind in (1, 0):
+        relay(0, x, kind).start()
+    for kind in (1, 0):
+        to_plane(1, x, kind).start()
     partner_shared_in().start()
-    loop(1, n, lambda r: tell(r).start())
-    loop(0, experts, lambda e: partner_in(e).start())
-    partner_shared_out().start()
-    loop(0, experts, lambda e: partner_out(e).start())
+    loop(0, early, lambda e: partner_in(e).start())
 
     def shared_first(b):
         pre = jnp.dot(xall[z, c, b], sin[...], preferred_element_type=jnp.float32)
@@ -427,11 +436,22 @@
     local_shared_in().wait()
     partner_shared_in().wait_recv()
     shared_first(x)
-    token_swap().wait_recv()
-    relay(0, ox).start()
-    loop(1, planes, lambda i: to_plane(i, ox).start())
+    for kind in (1, 0):
+        token_swap(kind).wait_recv()
+        relay(0, ox, kind).start()
+        to_plane(1, ox, kind).start()
+
+    def to_others(i):
+        for kind in (1, 0):
+            to_plane(i, x, kind).start()
+        for kind in (1, 0):
+            to_plane(i, ox, kind).start()
+
+    loop(2, planes, to_others)
+    loop(early, experts, lambda e: partner_in(e).start())
+    partner_shared_out().start()
+    loop(0, experts, lambda e: partner_out(e).start())
     shared_first(ox)
-    loop(1, n, lambda r: tell(r).wait_recv())
 
     before = jnp.where(
         lax.broadcasted_iota(jnp.int32, (tok_rows, tok_rows), 0)
@@ -440,10 +460,16 @@
         0.0,
     ).astype(jnp.bfloat16)
 
-    def first_stage(k, weights_wait):
+    def first_stage(k, turn, mine):
         i = lax.rem(k + 1, planes)
         p = lax.rem(z + i, planes)
-        turn = lax.rem(k, 2)
+        if not mine:
+            for kind in (1, 0):
+                for b in range(chips):
+                    to_plane(i, b, kind).wait_recv()
+                    relay(i, b, kind).start()
+        for b in range(chips):
+            relay(i, b, 1).wait_recv()
 
         ids = jnp.concatenate([meta[p, b, :picks] for b in range(dp)], axis=1)
         weights = jnp.concatenate([meta[p, b, picks:] for b in range(dp)], axis=1)
@@ -456,11 +482,11 @@
         gates[...] = jnp.concatenate(gate, axis=0)
         for b in range(dp):
             lanes = slice(b * tok_rows, (b + 1) * tok_rows)
-            mine = chosen[:, lanes]
+            named = chosen[:, lanes]
             earlier = jnp.dot(
-                mine.astype(jnp.bfloat16), before, preferred_element_type=jnp.float32
+                named.astype(jnp.bfloat16), before, preferred_element_type=jnp.float32
             )
-            keys[:, lanes] = jnp.where(mine > 0.5, earlier + float(b * CAP), -1.0).astype(
+            keys[:, lanes] = jnp.where(named > 0.5, earlier + float(b * CAP), -1.0).astype(
                 jnp.int32
             )
 
@@ -474,15 +500,8 @@
             gslot[turn, e] = jnp.broadcast_to(gate, gslot.shape[2:])
 
         loop(0, experts, choose)
-
-        @pl.when(i > 0)
-        def _():
-            for b in range(chips):
-                to_plane(lax.max(i, 1), b).wait_recv()
-                relay(i, b).start()
-
         for b in range(chips):
-            relay(i, b).wait_recv()
+            relay(i, b, 0).wait_recv()
         plane = xall[p].reshape(span, half)
         chosen_rows = jnp.dot(
             pick[turn].reshape(experts * slots, span), plane, preferred_element_type=jnp.float32
@@ -490,18 +509,23 @@
         rows[...] = chosen_rows.astype(jnp.bfloat16).reshape(rows.shape)
 
         def project(e):
-            if weights_wait:
+            if mine:
                 local_in(e).wait()
                 partner_in(e).wait_recv()
             pre = jnp.dot(rows[e], win[e], preferred_element_type=jnp.float32)
             send[k, e] = pre.astype(jnp.bfloat16)
+
+        def project_and_send(e):
+            project(e)
             swap(k, e).start()
 
-        loop(0, experts, project)
-
-    def second_stage(k):
-        turn = lax.rem(k, 2)
-
+        if mine:
+            loop(0, head, project_and_send)
+            loop(head, experts, project)
+        else:
+            loop(0, experts, project_and_send)
+
+    def second_stage(k, turn, first, end):
         def project(e):
             swap(k, e).wait_recv()
             total = send[k, e].astype(jnp.float32) + recv[k, e].astype(jnp.float32)
@@ -509,89 +533,113 @@
             result = jnp.dot(h, wout[e], preferred_element_type=jnp.float32)
             scaled[e] = (result * gslot[turn, e][:, :1]).astype(jnp.bfloat16)
 
-        loop(0, experts, project)
-
-        def combine(core):
-            lanes = start_of(core, own_rows)
-            return lax.dot_general(
-                pick[turn, :, :, lanes].reshape(experts * slots, own_rows),
-                scaled[...].reshape(experts * slots, half),
-                (((0,), (0,)), ((), ())),
-                preferred_element_type=jnp.float32,
-            )
-
-        psend[k] = combine(oc).astype(jnp.bfloat16)
-        pair(k).start()
-        own[...] = combine(c)
-        pair(k).wait_recv()
-        own[...] += precv[k].astype(jnp.float32)
-
-    def shared_second():
-        local_shared_out().wait()
-        partner_shared_out().wait_recv()
-        for b in range(chips):
-            shared_swap(b).wait_recv()
-        total = ssend[...].astype(jnp.float32) + srecv[...].astype(jnp.float32)
-        h = jax.nn.gelu(total).astype(jnp.bfloat16).reshape(own_rows, -1)
-        shared[...] = jnp.dot(h, sout[...], preferred_element_type=jnp.float32)
-
-    first_stage(0, True)
-    shared_second()
-    for e in range(experts):
+        loop(first, end, project)
+
+    def combine(turn, first, end, lanes, count):
+        return lax.dot_general(
+            pick[turn, first:end, :, lanes].reshape((end - first) * slots, count),
+            scaled[first:end].reshape((end - first) * slots, half),
+            (((0,), (0,)), ((), ())),
+            preferred_element_type=jnp.float32,
+        )
+
+    first_stage(last, 2, True)
+    first_stage(0, 0, False)
+
+    local_shared_out().wait()
+    partner_shared_out().wait_recv()
+    for b in range(chips):
+        shared_swap(b).wait_recv()
+    total = ssend[...].astype(jnp.float32) + srecv[...].astype(jnp.float32)
+    h = jax.nn.gelu(total).astype(jnp.bfloat16).reshape(own_rows, -1)
+    shared[...] = jnp.dot(h, sout[...], preferred_element_type=jnp.float32)
+
+    def out_weights(e):
         local_out(e).wait()
         partner_out(e).wait_recv()
 
+    loop(0, experts, out_weights)
+
+    second_stage(last, 2, 0, head)
+    own[...] = shared[...] + combine(2, 0, head, start_of(c, own_rows), own_rows)
+    other[...] = combine(2, 0, head, start_of(oc, own_rows), own_rows)
+
     def plane_step(k):
-        first_stage(k + 1, False)
-        second_stage(k)
-        zsend[k] = own[...].astype(jnp.bfloat16)
+        turn = lax.rem(k, 2)
+
+        @pl.when(k < last - 1)
+        def _():
+            first_stage(k + 1, lax.rem(k + 1, 2), False)
+
+        @pl.when(k == last - 1)
+        def _():
+            loop(head, experts, lambda e: swap(last, e).start())
+
+        second_stage(k, turn, 0, experts)
+        psend[k] = combine(turn, 0, experts, start_of(oc, own_rows), own_rows).astype(
+            jnp.bfloat16
+        )
+        pair(k).start()
+        mine = combine(turn, 0, experts, start_of(c, own_rows), own_rows)
+        pair(k).wait_recv()
+        zsend[k] = (mine + precv[k].astype(jnp.float32)).astype(jnp.bfloat16)
         give(k).start()
 
-    loop(0, planes - 1, plane_step)
-    second_stage(planes - 1)
-    total = own[...] + shared[...]
-    for k in range(planes - 1):
+    loop(0, last, plane_step)
+
+    second_stage(last, 2, head, experts)
+    for b in (ox, x):
+        lanes = start_of(oc * chips + b, tok_rows)
+        extra = combine(2, head, experts, lanes, tok_rows)
+        osend[b] = (other[start_of(b, tok_rows), :] + extra).astype(jnp.bfloat16)
+        own_pair(b).start()
+    total = own[...] + combine(2, head, experts, start_of(c, own_rows), own_rows)
+    for k in range(last):
         give(k).wait_recv()
         total = total + zrecv[k].astype(jnp.float32)
     own[...] = total
-    fsend[...] = own[start_of(ox, tok_rows), :].astype(jnp.bfloat16)
-    finish().start()
     mine = start_of(x, half)
     theirs = start_of(ox, half)
+    own_pair(ox).wait_recv()
+    fsend[...] = (own[start_of(ox, tok_rows), :] + orecv[ox].astype(jnp.float32)).astype(
+        jnp.bfloat16
+    )
+    finish().start()
+    own_pair(x).wait_recv()
     out_ref[:, mine] = (
-        tok_ref[:, mine].astype(jnp.float32) + own[start_of(x, tok_rows), :]
+        tok[:, mine].astype(jnp.float32)
+        + own[start_of(x, tok_rows), :]
+        + orecv[x].astype(jnp.float32)
     ).astype(out_ref.dtype)
-    finish().wait_recv()
-    out_ref[:, theirs] = (
-        tok_ref[:, theirs].astype(jnp.float32) + frecv[...].astype(jnp.float32)
-    ).astype(out_ref.dtype)
-
-    token_swap().wait_send()
+
+    for kind in (0, 1):
+        token_swap(kind).wait_send()
     partner_shared_in().wait_send()
     partner_shared_out().wait_send()
-    finish().wait_send()
-    loop(1, n, lambda r: tell(r).wait_send())
 
     def weights_sent(e):
         partner_in(e).wait_send()
         partner_out(e).wait_send()
+        loop(0, planes, lambda k: swap(k, e).wait_send())
 
     loop(0, experts, weights_sent)
     for b in range(chips):
         shared_swap(b).wait_send()
-
-        def sent(i):
-            relay(i, b).wait_send()
-
-        loop(0, planes, sent)
-        loop(1, planes, lambda i: to_plane(i, b).wait_send())
+        own_pair(b).wait_send()
+        for kind in (0, 1):
+            loop(0, planes, lambda i: relay(i, b, kind).wait_send())
+            loop(1, planes, lambda i: to_plane(i, b, kind).wait_send())
 
     def plane_sent(k):
-        loop(0, experts, lambda e: swap(k, e).wait_send())
         pair(k).wait_send()
-
-    loop(0, planes, plane_sent)
-    loop(0, planes - 1, lambda k: give(k).wait_send())
+        give(k).wait_send()
+
+    loop(0, last, plane_sent)
+
+    finish().wait()
+    out_ref[:, theirs] = (
+        tok[:, theirs].astype(jnp.float32) + frecv[...].astype(jnp.float32)
+    ).astype(out_ref.dtype)
 
 
 def fused(tokens, expert_ids, gate_weights, expert_in, expert_out, shared_in, shared_out):
@@ -604,10 +652,12 @@
     half = width // chips
     slots, span = dp * CAP, dp * tok_rows
     own_rows = chips * tok_rows
-    named = jnp.concatenate([expert_ids.astype(jnp.float32), gate_weights], axis=1).T
     bf16, f32 = jnp.bfloat16, jnp.float32
     vmem, dma = pltpu.VMEM, pltpu.SemaphoreType.DMA
     scratch = [
+        vmem((tok_rows, width), bf16),
+        vmem((picks, tok_rows), jnp.int32),
+        vmem((picks, tok_rows), f32),
         vmem((tok_rows, width), bf16),
         vmem((planes, cores, chips, tok_rows, half), bf16),
         vmem((planes, dp, 2 * picks, tok_rows), f32),
@@ -617,8 +667,8 @@
         vmem((hidden, half), bf16),
         vmem((experts, span), jnp.int32),
         vmem((experts, span), f32),
-        vmem((2, experts, slots, span), bf16),
-        vmem((2, experts, slots, 128), f32),
+        vmem((3, experts, slots, span), bf16),
+        vmem((3, experts, slots, 128), f32),
         vmem((experts, slots, half), bf16),
         vmem((planes, experts, slots, hidden), bf16),
         vmem((planes, experts, slots, hidden), bf16),
@@ -627,43 +677,43 @@
         vmem((own_rows, half), f32),
         vmem((experts, slots, half), bf16),
         vmem((own_rows, half), f32),
-        vmem((planes, own_rows, half), bf16),
-        vmem((planes, own_rows, half), bf16),
+        vmem((own_rows, half), f32),
+        vmem((planes - 1, own_rows, half), bf16),
+        vmem((planes - 1, own_rows, half), bf16),
+        vmem((chips, tok_rows, half), bf16),
+        vmem((chips, tok_rows, half), bf16),
         vmem((planes - 1, own_rows, half), bf16),
         vmem((planes - 1, own_rows, half), bf16),
         vmem((tok_rows, half), bf16),
         vmem((tok_rows, half), bf16),
+        dma((3,)),
         dma((2 * experts + 2,)),
-        dma((2 * experts + 2,)),
-        dma((2 * experts + 2,)),
-        dma((4,)),
-        dma((planes - 1, chips)),
-        dma((planes - 1, chips)),
-        dma((planes, chips)),
-        dma((planes, chips)),
-        dma((planes * dp,)),
-        dma((planes * dp,)),
-        dma((planes, experts)),
-        dma((planes, experts)),
-        dma((chips,)),
-        dma((chips,)),
-        dma((planes,)),
-        dma((planes,)),
-        dma((planes - 1,)),
-        dma((planes - 1,)),
     ]
-    whole = pl.BlockSpec(memory_space=pltpu.VMEM)
+    pairs = [
+        (2 * experts + 2,),
+        (2,),
+        (planes - 1, chips, 2),
+        (planes, chips, 2),
+        (planes, experts),
+        (chips,),
+        (planes - 1,),
+        (chips,),
+        (planes - 1,),
+        (1,),
+    ]
+    for shape in pairs:
+        scratch += [dma(shape), dma(shape)]
     apart = pl.BlockSpec(memory_space=pl.ANY)
     return pl.pallas_call(
         functools.partial(fused_kernel, (planes, chips, cores)),
-        in_specs=[whole, whole, apart, apart, apart, apart],
-        out_specs=whole,
+        in_specs=[apart] * 7,
+        out_specs=pl.BlockSpec(memory_space=pltpu.VMEM),
         out_shape=jax.ShapeDtypeStruct((tok_rows, width), tokens.dtype),
         scratch_shapes=scratch,
         compiler_params=pltpu.CompilerParams(
             collective_id=0, has_side_effects=True, vmem_limit_bytes=63 * 1024 * 1024
         ),
-    )(tokens, named, expert_in, expert_out, shared_in, shared_out)
+    )(tokens, expert_ids.T, gate_weights.T, expert_in, expert_out, shared_in, shared_out)
 
 
 def fits(mesh, args):

time: 142 us -> 127 us (0.89)
  Pallas kernels: 138 us -> 126 us
  other arithmetic: 1.97 us -> 0 us
    pallas_call x1, Pallas kernels: 138 us -> 126 us  [fused(): pl.pallas_call(functools.partial(fused_kernel, (planes, chips, cores)), i...]
where the time goes in v2:
time: 127 us
  Pallas kernels  126 us (99%)
  local copies, waits for them, and re-layouts  1.77 us (1%)
    pallas_call x1, Pallas kernels, fused(): pl.pallas_call(functools.partial(fused_kernel, (planes, chips, cores)), i...  126 us

profile of v2, /device:TPU:0, one launch (start us, length us, event | category | flops | bytes accessed | tf_op | source)
XLA Modules:
  0.0 127.4 jit_solution(8138637394944800036)
XLA Ops:
  0.0 125.6 %shard_map.73 = bf16[128,1536]{1,0:T(8,128)(2,1)} custom-call(bf16[128,1536]{1,0:T(8,128)(2,1)} %tok_hbm.1, s32[8,128]{1,0:T(8,128)} %bitcast.2, f32[8,128]{1,0:T(8,128)} %bitcast.3, bf16[16,384,768]{2,1,0:T(8,128)(2,1)} %win_hbm.1, bf16[16,768,384]{2,1,0:T(8,128)(2,1)} %wout_hbm.1, bf16[384,768]{1,0:T(8,128)(2,1)} %sin_hbm.1, bf16[768,384]{1,0:T(8,128)(2,1)} %sout_hbm.1), custom_call_target="tpu_custom_call" | custom-call | tf_op jit(solution)/shard_map/pallas_call | solution.py:707
  125.6 1.8 %copy.9 = bf16[128,1536]{1,0:T(8,128)(2,1)} copy(bf16[128,1536]{1,0:T(8,128)(2,1)} %shard_map.73) | data formatting | bytes 786432

commit v3 on v2

--- a/solution.py
+++ b/solution.py
@@ -192,7 +192,13 @@
     return pl.ds(pl.multiple_of(index * size, size), size)
 
 
-HEAD = 4
+HEAD = 3
+
+
+def plane_orders(planes):
+    if planes == 4:
+        return ((1, 2, 1, 2), (3, 3, 0, 0), (2, 0, 3, 1))
+    return tuple(tuple((z + k) % planes for z in range(planes)) for k in range(1, planes))
 
 
 def fused_kernel(
@@ -224,7 +230,6 @@
     recv,
     ssend,
     srecv,
-    shared,
     scaled,
     own,
     other,
@@ -270,7 +275,8 @@
     slots, span = pick.shape[2:]
     own_rows = chips * tok_rows
     last = planes - 1
-    head = min(HEAD, experts)
+    head = min(HEAD, experts // 2)
+    close = max(experts - 2, head + 1)
 
     z = lax.axis_index("expert")
     d = lax.axis_index("dp")
@@ -299,8 +305,15 @@
 
         lax.fori_loop(first, end, step, 0)
 
-    def plane_at(i):
-        return {"expert": lax.rem(z + i, planes)}
+    orders = plane_orders(planes)
+
+    def at_step(k):
+        found = 0
+        for step, order in enumerate(orders):
+            for place, p in enumerate(order):
+                hit = jnp.logical_and(k == step, z == place)
+                found = jnp.where(hit, p, found)
+        return jnp.where(k == last, z, found)
 
     def local_in(e):
         return pltpu.make_async_copy(
@@ -365,15 +378,29 @@
         src = meta.at[z, c * chips + x] if kind else norm.at[:, start_of(ox, half)]
         return remote(src, block(z, x, kind), xssem.at[kind], xrsem.at[kind], across)
 
-    def to_plane(i, b, kind):
+    def to_plane(p, b, kind):
         ref = block(z, b, kind)
         return remote(
-            ref, ref, zssem.at[i - 1, b, kind], zrsem.at[i - 1, b, kind], plane_at(planes - i)
-        )
-
-    def relay(i, b, kind):
-        ref = block(lax.rem(z + i, planes), b, kind)
-        return remote(ref, ref, rssem.at[i, b, kind], rrsem.at[i, b, kind], partner)
+            ref, ref, zssem.at[p, b, kind], zrsem.at[z, b, kind], {"expert": p}
+        )
+
+    def from_plane(p, b, kind):
+        ref = block(p, b, kind)
+        return remote(
+            ref, ref, zssem.at[p, b, kind], zrsem.at[p, b, kind], {"expert": p}
+        )
+
+    def send_tokens(k, b):
+        for p in range(planes):
+
+            @pl.when(z == orders[k][p])
+            def _():
+                for kind in (1, 0):
+                    to_plane(p, b, kind).start()
+
+    def relay(p, b, kind):
+        ref = block(p, b, kind)
+        return remote(ref, ref, rssem.at[p, b, kind], rrsem.at[p, b, kind], partner)
 
     def swap(k, e):
         return remote(send.at[k, e], recv.at[k, e], pssem.at[k, e], prsem.at[k, e], across)
@@ -388,13 +415,19 @@
         return remote(osend.at[b], orecv.at[b], bssem.at[b], brsem.at[b], partner)
 
     def give(k):
-        return remote(zsend.at[k], zrecv.at[k], ossem.at[k], orsem.at[k], plane_at(k + 1))
+        return remote(
+            zsend.at[k], zrecv.at[z], ossem.at[k], orsem.at[z], {"expert": at_step(k)}
+        )
+
+    def given(p):
+        return remote(zsend.at[0], zrecv.at[p], ossem.at[0], orsem.at[p], {"expert": p})
 
     def finish():
         return remote(fsend, frecv, fssem.at[0], frsem.at[0], across)
 
     barrier = pltpu.get_barrier_semaphore()
-    for device in [across, partner] + [plane_at(i) for i in range(1, planes)]:
+    peers = [{"expert": lax.rem(z + i, planes)} for i in range(1, planes)]
+    for device in [across, partner] + peers:
         pl.semaphore_signal(barrier, inc=1, device_id=device, device_id_type=mesh_ids)
     read_tok = pltpu.make_async_copy(tok_hbm, tok, isem.at[0])
     read_ids = pltpu.make_async_copy(ids_hbm, ids_in, isem.at[1])
@@ -422,36 +455,28 @@
     for kind in (1, 0):
         token_swap(kind).start()
     for kind in (1, 0):
-        relay(0, x, kind).start()
-    for kind in (1, 0):
-        to_plane(1, x, kind).start()
+        relay(z, x, kind).start()
+    send_tokens(0, x)
     partner_shared_in().start()
     loop(0, early, lambda e: partner_in(e).start())
 
     def shared_first(b):
         pre = jnp.dot(xall[z, c, b], sin[...], preferred_element_type=jnp.float32)
         ssend[b] = pre.astype(jnp.bfloat16)
-        shared_swap(b).start()
 
     local_shared_in().wait()
     partner_shared_in().wait_recv()
     shared_first(x)
+    shared_swap(x).start()
     for kind in (1, 0):
         token_swap(kind).wait_recv()
-        relay(0, ox, kind).start()
-        to_plane(1, ox, kind).start()
-
-    def to_others(i):
-        for kind in (1, 0):
-            to_plane(i, x, kind).start()
-        for kind in (1, 0):
-            to_plane(i, ox, kind).start()
-
-    loop(2, planes, to_others)
+        relay(z, ox, kind).start()
+    send_tokens(0, ox)
     loop(early, experts, lambda e: partner_in(e).start())
     partner_shared_out().start()
     loop(0, experts, lambda e: partner_out(e).start())
     shared_first(ox)
+    shared_swap(ox).start()
 
     before = jnp.where(
         lax.broadcasted_iota(jnp.int32, (tok_rows, tok_rows), 0)
@@ -461,15 +486,21 @@
     ).astype(jnp.bfloat16)
 
     def first_stage(k, turn, mine):
-        i = lax.rem(k + 1, planes)
-        p = lax.rem(z + i, planes)
+        p = z if mine else at_step(k)
         if not mine:
             for kind in (1, 0):
                 for b in range(chips):
-                    to_plane(i, b, kind).wait_recv()
-                    relay(i, b, kind).start()
+                    from_plane(p, b, kind).wait_recv()
+                    relay(p, b, kind).start()
+            for step in range(1, last):
+
+                @pl.when(k == step - 1)
+                def _():
+                    for b in (x, ox):
+                        send_tokens(step, b)
+
         for b in range(chips):
-            relay(i, b, 1).wait_recv()
+            relay(p, b, 1).wait_recv()
 
         ids = jnp.concatenate([meta[p, b, :picks] for b in range(dp)], axis=1)
         weights = jnp.concatenate([meta[p, b, picks:] for b in range(dp)], axis=1)
@@ -501,7 +532,7 @@
 
         loop(0, experts, choose)
         for b in range(chips):
-            relay(i, b, 0).wait_recv()
+            relay(p, b, 0).wait_recv()
         plane = xall[p].reshape(span, half)
         chosen_rows = jnp.dot(
             pick[turn].reshape(experts * slots, span), plane, preferred_element_type=jnp.float32
@@ -548,11 +579,14 @@
 
     local_shared_out().wait()
     partner_shared_out().wait_recv()
-    for b in range(chips):
+
+    def shared_second(b):
         shared_swap(b).wait_recv()
-    total = ssend[...].astype(jnp.float32) + srecv[...].astype(jnp.float32)
-    h = jax.nn.gelu(total).astype(jnp.bfloat16).reshape(own_rows, -1)
-    shared[...] = jnp.dot(h, sout[...], preferred_element_type=jnp.float32)
+        total = ssend[b].astype(jnp.float32) + srecv[b].astype(jnp.float32)
+        h = jax.nn.gelu(total).astype(jnp.bfloat16)
+        own[start_of(b, tok_rows), :] += jnp.dot(
+            h, sout[...], preferred_element_type=jnp.float32
+        )
 
     def out_weights(e):
         local_out(e).wait()
@@ -561,8 +595,10 @@
     loop(0, experts, out_weights)
 
     second_stage(last, 2, 0, head)
-    own[...] = shared[...] + combine(2, 0, head, start_of(c, own_rows), own_rows)
+    own[...] = combine(2, 0, head, start_of(c, own_rows), own_rows)
     other[...] = combine(2, 0, head, start_of(oc, own_rows), own_rows)
+    for b in range(chips):
+        shared_second(b)
 
     def plane_step(k):
         turn = lax.rem(k, 2)
@@ -587,16 +623,20 @@
 
     loop(0, last, plane_step)
 
-    second_stage(last, 2, head, experts)
+    second_stage(last, 2, head, close)
+    own[...] += combine(2, head, close, start_of(c, own_rows), own_rows)
+    other[...] += combine(2, head, close, start_of(oc, own_rows), own_rows)
+    second_stage(last, 2, close, experts)
     for b in (ox, x):
         lanes = start_of(oc * chips + b, tok_rows)
-        extra = combine(2, head, experts, lanes, tok_rows)
+        extra = combine(2, close, experts, lanes, tok_rows)
         osend[b] = (other[start_of(b, tok_rows), :] + extra).astype(jnp.bfloat16)
         own_pair(b).start()
-    total = own[...] + combine(2, head, experts, start_of(c, own_rows), own_rows)
-    for k in range(last):
-        give(k).wait_recv()
-        total = total + zrecv[k].astype(jnp.float32)
+    total = own[...] + combine(2, close, experts, start_of(c, own_rows), own_rows)
+    for r in range(1, planes):
+        p = lax.rem(z + r, planes)
+        given(p).wait_recv()
+        total = total + zrecv[p].astype(jnp.float32)
     own[...] = total
     mine = start_of(x, half)
     theirs = start_of(ox, half)
@@ -627,8 +667,12 @@
         shared_swap(b).wait_send()
         own_pair(b).wait_send()
         for kind in (0, 1):
-            loop(0, planes, lambda i: relay(i, b, kind).wait_send())
-            loop(1, planes, lambda i: to_plane(i, b, kind).wait_send())
+            loop(0, planes, lambda p: relay(p, b, kind).wait_send())
+            loop(
+                1,
+                planes,
+                lambda r: to_plane(lax.rem(z + r, planes), b, kind).wait_send(),
+            )
 
     def plane_sent(k):
         pair(k).wait_send()
@@ -674,7 +718,6 @@
         vmem((planes, experts, slots, hidden), bf16),
         vmem((chips, tok_rows, hidden), bf16),
         vmem((chips, tok_rows, hidden), bf16),
-        vmem((own_rows, half), f32),
         vmem((experts, slots, half), bf16),
         vmem((own_rows, half), f32),
         vmem((own_rows, half), f32),
@@ -683,7 +726,7 @@
         vmem((chips, tok_rows, half), bf16),
         vmem((chips, tok_rows, half), bf16),
         vmem((planes - 1, own_rows, half), bf16),
-        vmem((planes - 1, own_rows, half), bf16),
+        vmem((planes, own_rows, half), bf16),
         vmem((tok_rows, half), bf16),
         vmem((tok_rows, half), bf16),
         dma((3,)),
@@ -692,13 +735,13 @@
     pairs = [
         (2 * experts + 2,),
         (2,),
-        (planes - 1, chips, 2),
+        (planes, chips, 2),
         (planes, chips, 2),
         (planes, experts),
         (chips,),
         (planes - 1,),
         (chips,),
-        (planes - 1,),
+        (planes,),
         (1,),
     ]
     for shape in pairs:

time: 127 us -> 116 us (0.913)
  Pallas kernels: 126 us -> 114 us
    pallas_call x1, Pallas kernels: 126 us -> 114 us  [fused(): pl.pallas_call(functools.partial(fused_kernel, (planes, chips, cores)), i...]
where the time goes in v3:
time: 116 us
  Pallas kernels  114 us (98%)
  local copies, waits for them, and re-layouts  1.77 us (2%)
    pallas_call x1, Pallas kernels, fused(): pl.pallas_call(functools.partial(fused_kernel, (planes, chips, cores)), i...  114 us

profile of v3, /device:TPU:0, one launch (start us, length us, event | category | flops | bytes accessed | tf_op | source)
XLA Modules:
  0.0 116.2 jit_solution(7124312558312624277)
XLA Ops:
  0.0 114.5 %shard_map.73 = bf16[128,1536]{1,0:T(8,128)(2,1)} custom-call(bf16[128,1536]{1,0:T(8,128)(2,1)} %tok_hbm.1, s32[8,128]{1,0:T(8,128)} %bitcast.2, f32[8,128]{1,0:T(8,128)} %bitcast.3, bf16[16,384,768]{2,1,0:T(8,128)(2,1)} %win_hbm.1, bf16[16,768,384]{2,1,0:T(8,128)(2,1)} %wout_hbm.1, bf16[384,768]{1,0:T(8,128)(2,1)} %sin_hbm.1, bf16[768,384]{1,0:T(8,128)(2,1)} %sout_hbm.1), custom_call_target="tpu_custom_call" | custom-call | tf_op jit(solution)/shard_map/pallas_call | solution.py:750
  114.5 1.8 %copy.9 = bf16[128,1536]{1,0:T(8,128)(2,1)} copy(bf16[128,1536]{1,0:T(8,128)(2,1)} %shard_map.73) | data formatting | bytes 786432

commit v4 on v3

--- a/solution.py
+++ b/solution.py
@@ -276,7 +276,7 @@
     own_rows = chips * tok_rows
     last = planes - 1
     head = min(HEAD, experts // 2)
-    close = max(experts - 2, head + 1)
+    close = max(experts - 1, head + 1)
 
     z = lax.axis_index("expert")
     d = lax.axis_index("dp")
@@ -315,60 +315,50 @@
                 found = jnp.where(hit, p, found)
         return jnp.where(k == last, z, found)
 
-    def local_in(e):
+    def mine_of(core):
+        return pl.ds(core * experts, experts)
+
+    def local_in():
         return pltpu.make_async_copy(
-            win_hbm.at[c * experts + e], win.at[e, start_of(c, part)], lsem.at[e]
-        )
-
-    def local_out(e):
+            win_hbm.at[mine_of(c)], win.at[:, start_of(c, part)], lsem.at[0]
+        )
+
+    def local_out():
         return pltpu.make_async_copy(
-            wout_hbm.at[c * experts + e],
-            wout.at[e, :, start_of(c, part)],
-            lsem.at[experts + e],
+            wout_hbm.at[mine_of(c)], wout.at[:, :, start_of(c, part)], lsem.at[1]
         )
 
     def local_shared_in():
-        return pltpu.make_async_copy(sin_hbm, sin.at[start_of(c, part)], lsem.at[2 * experts])
+        return pltpu.make_async_copy(sin_hbm, sin.at[start_of(c, part)], lsem.at[2])
 
     def local_shared_out():
-        return pltpu.make_async_copy(
-            sout_hbm, sout.at[:, start_of(c, part)], lsem.at[2 * experts + 1]
-        )
-
-    def partner_in(e):
+        return pltpu.make_async_copy(sout_hbm, sout.at[:, start_of(c, part)], lsem.at[3])
+
+    def partner_in(group):
+        first, count = ((0, head), (head, experts - head))[group]
         return remote(
-            win_hbm.at[oc * experts + e],
-            win.at[e, start_of(c, part)],
-            wssem.at[e],
-            wrsem.at[e],
+            win_hbm.at[pl.ds(oc * experts + first, count)],
+            win.at[pl.ds(first, count), start_of(c, part)],
+            wssem.at[group],
+            wrsem.at[group],
             partner,
         )
 
-    def partner_out(e):
+    def partner_out():
         return remote(
-            wout_hbm.at[oc * experts + e],
-            wout.at[e, :, start_of(c, part)],
-            wssem.at[experts + e],
-            wrsem.at[experts + e],
+            wout_hbm.at[mine_of(oc)],
+            wout.at[:, :, start_of(c, part)],
+            wssem.at[2],
+            wrsem.at[2],
             partner,
         )
 
     def partner_shared_in():
-        return remote(
-            sin_hbm,
-            sin.at[start_of(c, part)],
-            wssem.at[2 * experts],
-            wrsem.at[2 * experts],
-            partner,
-        )
+        return remote(sin_hbm, sin.at[start_of(c, part)], wssem.at[3], wrsem.at[3], partner)
 
     def partner_shared_out():
         return remote(
-            sout_hbm,
-            sout.at[:, start_of(c, part)],
-            wssem.at[2 * experts + 1],
-            wrsem.at[2 * experts + 1],
-            partner,
+            sout_hbm, sout.at[:, start_of(c, part)], wssem.at[4], wrsem.at[4], partner
         )
 
     def block(p, b, kind):
@@ -378,17 +368,16 @@
         src = meta.at[z, c * chips + x] if kind else norm.at[:, start_of(ox, half)]
         return remote(src, block(z, x, kind), xssem.at[kind], xrsem.at[kind], across)
 
+    def both(p, kind):
+        return meta.at[p, pl.ds(c * chips, chips)] if kind else xall.at[p, c]
+
     def to_plane(p, b, kind):
         ref = block(z, b, kind)
-        return remote(
-            ref, ref, zssem.at[p, b, kind], zrsem.at[z, b, kind], {"expert": p}
-        )
-
-    def from_plane(p, b, kind):
-        ref = block(p, b, kind)
-        return remote(
-            ref, ref, zssem.at[p, b, kind], zrsem.at[p, b, kind], {"expert": p}
-        )
+        return remote(ref, ref, zssem.at[kind], zrsem.at[z, kind], {"expert": p})
+
+    def from_plane(p, kind):
+        ref = both(p, kind)
+        return remote(ref, ref, zssem.at[kind], zrsem.at[p, kind], {"expert": p})
 
     def send_tokens(k, b):
         for p in range(planes):
@@ -398,29 +387,37 @@
                 for kind in (1, 0):
                     to_plane(p, b, kind).start()
 
-    def relay(p, b, kind):
-        ref = block(p, b, kind)
-        return remote(ref, ref, rssem.at[p, b, kind], rrsem.at[p, b, kind], partner)
+    def relay_block(b, kind):
+        ref = block(z, b, kind)
+        return remote(ref, ref, rssem.at[kind], rrsem.at[z, kind], partner)
+
+    def relay(p, kind):
+        ref = both(p, kind)
+        return remote(ref, ref, rssem.at[kind], rrsem.at[p, kind], partner)
+
+    def tokens_sent(kind, count, s_sem):
+        ref = meta.at[pl.ds(0, count), pl.ds(0, chips)] if kind else xall.at[pl.ds(0, count), 0]
+        return remote(ref, ref, s_sem.at[kind], zrsem.at[0, kind], partner)
 
     def swap(k, e):
-        return remote(send.at[k, e], recv.at[k, e], pssem.at[k, e], prsem.at[k, e], across)
+        return remote(send.at[k, e], recv.at[k, e], pssem.at[0], prsem.at[k, e], across)
 
     def shared_swap(b):
-        return remote(ssend.at[b], srecv.at[b], ssem.at[b], srsem.at[b], across)
+        return remote(ssend.at[b], srecv.at[b], ssem.at[0], srsem.at[b], across)
 
     def pair(k):
-        return remote(psend.at[k], precv.at[k], dssem.at[k], drsem.at[k], partner)
+        return remote(psend.at[k], precv.at[k], dssem.at[0], drsem.at[k], partner)
 
     def own_pair(b):
-        return remote(osend.at[b], orecv.at[b], bssem.at[b], brsem.at[b], partner)
+        return remote(osend.at[b], orecv.at[b], bssem.at[0], brsem.at[b], partner)
 
     def give(k):
         return remote(
-            zsend.at[k], zrecv.at[z], ossem.at[k], orsem.at[z], {"expert": at_step(k)}
-        )
-
-    def given(p):
-        return remote(zsend.at[0], zrecv.at[p], ossem.at[0], orsem.at[p], {"expert": p})
+            zsend.at[k], zrecv.at[z], ossem.at[0], orsem.at[0], {"expert": at_step(k)}
+        )
+
+    def given():
+        return remote(zsend, zrecv.at[pl.ds(0, last)], ossem.at[0], orsem.at[0], partner)
 
     def finish():
         return remote(fsend, frecv, fssem.at[0], frsem.at[0], across)
@@ -436,9 +433,9 @@
     read_ids.start()
     read_gate.start()
     local_shared_in().start()
-    loop(0, experts, lambda e: local_in(e).start())
+    local_in().start()
     local_shared_out().start()
-    loop(0, experts, lambda e: local_out(e).start())
+    local_out().start()
     read_ids.wait()
     read_gate.wait()
     meta[z, c * chips + x, :picks] = ids_in[...].astype(jnp.float32)
@@ -451,14 +448,13 @@
     xall[z, c, x] = norm[:, start_of(x, half)]
 
     pl.semaphore_wait(barrier, planes + 1)
-    early = min(3, experts)
     for kind in (1, 0):
         token_swap(kind).start()
+    partner_shared_in().start()
     for kind in (1, 0):
-        relay(z, x, kind).start()
+        relay_block(x, kind).start()
     send_tokens(0, x)
-    partner_shared_in().start()
-    loop(0, early, lambda e: partner_in(e).start())
+    partner_in(0).start()
 
     def shared_first(b):
         pre = jnp.dot(xall[z, c, b], sin[...], preferred_element_type=jnp.float32)
@@ -470,11 +466,11 @@
     shared_swap(x).start()
     for kind in (1, 0):
         token_swap(kind).wait_recv()
-        relay(z, ox, kind).start()
+        relay_block(ox, kind).start()
     send_tokens(0, ox)
-    loop(early, experts, lambda e: partner_in(e).start())
+    partner_in(1).start()
     partner_shared_out().start()
-    loop(0, experts, lambda e: partner_out(e).start())
+    partner_out().start()
     shared_first(ox)
     shared_swap(ox).start()
 
@@ -489,9 +485,8 @@
         p = z if mine else at_step(k)
         if not mine:
             for kind in (1, 0):
-                for b in range(chips):
-                    from_plane(p, b, kind).wait_recv()
-                    relay(p, b, kind).start()
+                from_plane(p, kind).wait_recv()
+                relay(p, kind).start()
             for step in range(1, last):
 
                 @pl.when(k == step - 1)
@@ -499,8 +494,7 @@
                     for b in (x, ox):
                         send_tokens(step, b)
 
-        for b in range(chips):
-            relay(p, b, 1).wait_recv()
+        relay(p, 1).wait_recv()
 
         ids = jnp.concatenate([meta[p, b, :picks] for b in range(dp)], axis=1)
         weights = jnp.concatenate([meta[p, b, picks:] for b in range(dp)], axis=1)
@@ -531,8 +525,7 @@
             gslot[turn, e] = jnp.broadcast_to(gate, gslot.shape[2:])
 
         loop(0, experts, choose)
-        for b in range(chips):
-            relay(p, b, 0).wait_recv()
+        relay(p, 0).wait_recv()
         plane = xall[p].reshape(span, half)
         chosen_rows = jnp.dot(
             pick[turn].reshape(experts * slots, span), plane, preferred_element_type=jnp.float32
@@ -540,9 +533,6 @@
         rows[...] = chosen_rows.astype(jnp.bfloat16).reshape(rows.shape)
 
         def project(e):
-            if mine:
-                local_in(e).wait()
-                partner_in(e).wait_recv()
             pre = jnp.dot(rows[e], win[e], preferred_element_type=jnp.float32)
             send[k, e] = pre.astype(jnp.bfloat16)
 
@@ -551,7 +541,10 @@
             swap(k, e).start()
 
         if mine:
+            local_in().wait()
+            partner_in(0).wait_recv()
             loop(0, head, project_and_send)
+            partner_in(1).wait_recv()
             loop(head, experts, project)
         else:
             loop(0, experts, project_and_send)
@@ -588,11 +581,8 @@
             h, sout[...], preferred_element_type=jnp.float32
         )
 
-    def out_weights(e):
-        local_out(e).wait()
-        partner_out(e).wait_recv()
-
-    loop(0, experts, out_weights)
+    local_out().wait()
+    partner_out().wait_recv()
 
     second_stage(last, 2, 0, head)
     own[...] = combine(2, 0, head, start_of(c, own_rows), own_rows)
@@ -633,10 +623,9 @@
         osend[b] = (other[start_of(b, tok_rows), :] + extra).astype(jnp.bfloat16)
         own_pair(b).start()
     total = own[...] + combine(2, close, experts, start_of(c, own_rows), own_rows)
+    given().wait_recv()
     for r in range(1, planes):
-        p = lax.rem(z + r, planes)
-        given(p).wait_recv()
-        total = total + zrecv[p].astype(jnp.float32)
+        total = total + zrecv[lax.rem(z + r, planes)].astype(jnp.float32)
     own[...] = total
     mine = start_of(x, half)
     theirs = start_of(ox, half)
@@ -654,31 +643,17 @@
 
     for kind in (0, 1):
         token_swap(kind).wait_send()
+        tokens_sent(kind, last, zssem).wait_send()
+        tokens_sent(kind, planes, rssem).wait_send()
+        partner_in(kind).wait_send()
     partner_shared_in().wait_send()
     partner_shared_out().wait_send()
-
-    def weights_sent(e):
-        partner_in(e).wait_send()
-        partner_out(e).wait_send()
-        loop(0, planes, lambda k: swap(k, e).wait_send())
-
-    loop(0, experts, weights_sent)
-    for b in range(chips):
-        shared_swap(b).wait_send()
-        own_pair(b).wait_send()
-        for kind in (0, 1):
-            loop(0, planes, lambda p: relay(p, b, kind).wait_send())
-            loop(
-                1,
-                planes,
-                lambda r: to_plane(lax.rem(z + r, planes), b, kind).wait_send(),
-            )
-
-    def plane_sent(k):
-        pair(k).wait_send()
-        give(k).wait_send()
-
-    loop(0, last, plane_sent)
+    partner_out().wait_send()
+    remote(send, recv, pssem.at[0], prsem.at[0, 0], across).wait_send()
+    remote(ssend, srecv, ssem.at[0], srsem.at[0], across).wait_send()
+    remote(osend, orecv, bssem.at[0], brsem.at[0], partner).wait_send()
+    remote(psend, precv, dssem.at[0], drsem.at[0], partner).wait_send()
+    given().wait_send()
 
     finish().wait()
     out_ref[:, theirs] = (
@@ -730,22 +705,22 @@
         vmem((tok_rows, half), bf16),
         vmem((tok_rows, half), bf16),
         dma((3,)),
-        dma((2 * experts + 2,)),
+        dma((4,)),
     ]
     pairs = [
-        (2 * experts + 2,),
-        (2,),
-        (planes, chips, 2),
-        (planes, chips, 2),
-        (planes, experts),
-        (chips,),
-        (planes - 1,),
-        (chips,),
-        (planes,),
-        (1,),
+        ((5,), (5,)),
+        ((2,), (2,)),
+        ((2,), (planes, 2)),
+        ((2,), (planes, 2)),
+        ((1,), (planes, experts)),
+        ((1,), (chips,)),
+        ((1,), (planes - 1,)),
+        ((1,), (chips,)),
+        ((1,), (1,)),
+        ((1,), (1,)),
     ]
-    for shape in pairs:
-        scratch += [dma(shape), dma(shape)]
+    for sent, received in pairs:
+        scratch += [dma(sent), dma(received)]
     apart = pl.BlockSpec(memory_space=pl.ANY)
     return pl.pallas_call(
         functools.partial(fused_kernel, (planes, chips, cores)),
@@ -754,7 +729,7 @@
         out_shape=jax.ShapeDtypeStruct((tok_rows, width), tokens.dtype),
         scratch_shapes=scratch,
         compiler_params=pltpu.CompilerParams(
-            collective_id=0, has_side_effects=True, vmem_limit_bytes=63 * 1024 * 1024
+            collective_id=0, has_side_effects=True, vmem_limit_bytes=56098816
         ),
     )(tokens, expert_ids.T, gate_weights.T, expert_in, expert_out, shared_in, shared_out)
 

time: 116 us -> 115 us (level)
  Pallas kernels: 114 us -> 112 us
    pallas_call x1, Pallas kernels: 114 us -> 112 us  [fused(): pl.pallas_call(functools.partial(fused_kernel, (planes, chips, cores)), i...]
where the time goes in v4:
time: 115 us
  Pallas kernels  112 us (97%)
  local copies, waits for them, and re-layouts  2.12 us (2%)
    pallas_call x1, Pallas kernels, fused(): pl.pallas_call(functools.partial(fused_kernel, (planes, chips, cores)), i...  112 us

profile of v4, /device:TPU:0, one launch (start us, length us, event | category | flops | bytes accessed | tf_op | source)
XLA Modules:
  0.0 114.5 jit_solution(7602643529015866377)
XLA Ops:
  0.0 0.0 copy-start
  0.0 0.7 copy-done
  0.7 0.0 copy-start.1
  0.7 0.7 copy-done.1
  1.4 112.4 %shard_map.73 = bf16[128,1536]{1,0:T(8,128)(2,1)S(1)} custom-call(bf16[128,1536]{1,0:T(8,128)(2,1)} %tok_hbm.1, s32[8,128]{1,0:T(8,128)S(1)} %bitcast.2, f32[8,128]{1,0:T(8,128)S(1)} %bitcast.3, bf16[16,384,768]{2,1,0:T(8,128)(2,1)} %win_hbm.1, bf16[16,768,384]{2,1,0:T(8,128)(2,1)} %wout_hbm.1, bf16[384,768]{1,0:T(8,128)(2,1)} %sin_hbm.1, ...), custom_call_target="tpu_custom_call" | custom-call | tf_op jit(solution)/shard_map/pallas_call | solution.py:725
  113.8 0.7 copy.9
Async XLA Ops:
  0.0 0.7 copy-start
  0.7 0.7 copy-start.1

commit v5 on v4

--- a/solution.py
+++ b/solution.py
@@ -453,8 +453,8 @@
     partner_shared_in().start()
     for kind in (1, 0):
         relay_block(x, kind).start()
+    partner_in(0).start()
     send_tokens(0, x)
-    partner_in(0).start()
 
     def shared_first(b):
         pre = jnp.dot(xall[z, c, b], sin[...], preferred_element_type=jnp.float32)
@@ -721,6 +721,8 @@
     ]
     for sent, received in pairs:
         scratch += [dma(sent), dma(received)]
+    given = (tokens, expert_ids.T, gate_weights.T, expert_in, expert_out, shared_in, shared_out)
+    given = [pltpu.with_memory_space_constraint(a, pltpu.HBM) for a in given]
     apart = pl.BlockSpec(memory_space=pl.ANY)
     return pl.pallas_call(
         functools.partial(fused_kernel, (planes, chips, cores)),
@@ -731,7 +733,7 @@
         compiler_params=pltpu.CompilerParams(
             collective_id=0, has_side_effects=True, vmem_limit_bytes=56098816
         ),
-    )(tokens, expert_ids.T, gate_weights.T, expert_in, expert_out, shared_in, shared_out)
+    )(*given)
 
 
 def fits(mesh, args):

time: 115 us -> 113 us (0.983)
  local copies, waits for them, and re-layouts: 2.12 us -> 0.75 us
    unnamed x5 -> x1, local copies, waits for them, and re-layouts: 2.12 us -> 0.75 us
where the time goes in v5:
time: 113 us
  Pallas kernels  112 us (99%)
    pallas_call x1, Pallas kernels, fused(): pl.pallas_call(functools.partial(fused_kernel, (planes, chips, cores)), i...  112 us

profile of v5, /device:TPU:0, one launch (start us, length us, event | category | flops | bytes accessed | tf_op | source)
XLA Modules:
  0.0 113.1 jit_solution(12803465080655928238)
XLA Ops:
  0.0 112.4 %shard_map.73 = bf16[128,1536]{1,0:T(8,128)(2,1)S(1)} custom-call(bf16[128,1536]{1,0:T(8,128)(2,1)} %tok_hbm.1, s32[8,128]{1,0:T(8,128)} %bitcast.2, f32[8,128]{1,0:T(8,128)} %bitcast.3, bf16[16,384,768]{2,1,0:T(8,128)(2,1)} %win_hbm.1, bf16[16,768,384]{2,1,0:T(8,128)(2,1)} %wout_hbm.1, bf16[384,768]{1,0:T(8,128)(2,1)} %sin_hbm.1, bf16[768,384]{1,0:T(8,128)(2,1)} %sout_hbm.1), custom_call_target="tpu_custom_call" | custom-call | tf_op jit(solution)/shard_map/pallas_call | solution.py:727
  112.4 0.7 copy.9

commit v6 on v5

--- a/solution.py
+++ b/solution.py
@@ -192,7 +192,7 @@
     return pl.ds(pl.multiple_of(index * size, size), size)
 
 
-HEAD = 3
+HEAD = 2
 
 
 def plane_orders(planes):
@@ -469,8 +469,6 @@
         relay_block(ox, kind).start()
     send_tokens(0, ox)
     partner_in(1).start()
-    partner_shared_out().start()
-    partner_out().start()
     shared_first(ox)
     shared_swap(ox).start()
 
@@ -481,12 +479,15 @@
         0.0,
     ).astype(jnp.bfloat16)
 
-    def first_stage(k, turn, mine):
+    def first_stage(k, turn, mine, weights_next=False):
         p = z if mine else at_step(k)
         if not mine:
             for kind in (1, 0):
                 from_plane(p, kind).wait_recv()
                 relay(p, kind).start()
+            if weights_next:
+                partner_shared_out().start()
+                partner_out().start()
             for step in range(1, last):
 
                 @pl.when(k == step - 1)
@@ -568,7 +569,7 @@
         )
 
     first_stage(last, 2, True)
-    first_stage(0, 0, False)
+    first_stage(0, 0, False, True)
 
     local_shared_out().wait()
     partner_shared_out().wait_recv()
@@ -616,29 +617,32 @@
     second_stage(last, 2, head, close)
     own[...] += combine(2, head, close, start_of(c, own_rows), own_rows)
     other[...] += combine(2, head, close, start_of(oc, own_rows), own_rows)
-    second_stage(last, 2, close, experts)
-    for b in (ox, x):
-        lanes = start_of(oc * chips + b, tok_rows)
-        extra = combine(2, close, experts, lanes, tok_rows)
-        osend[b] = (other[start_of(b, tok_rows), :] + extra).astype(jnp.bfloat16)
-        own_pair(b).start()
-    total = own[...] + combine(2, close, experts, start_of(c, own_rows), own_rows)
     given().wait_recv()
     for r in range(1, planes):
-        total = total + zrecv[lax.rem(z + r, planes)].astype(jnp.float32)
-    own[...] = total
+        own[...] += zrecv[lax.rem(z + r, planes)].astype(jnp.float32)
+    second_stage(last, 2, close, experts)
+
+    def last_part(core, b):
+        lanes = start_of(core * chips + b, tok_rows)
+        return combine(2, close, experts, lanes, tok_rows)
+
+    def to_partner(b):
+        total = other[start_of(b, tok_rows), :] + last_part(oc, b)
+        osend[b] = total.astype(jnp.bfloat16)
+        own_pair(b).start()
+
     mine = start_of(x, half)
     theirs = start_of(ox, half)
+    to_partner(ox)
+    total = own[start_of(ox, tok_rows), :] + last_part(c, ox)
     own_pair(ox).wait_recv()
-    fsend[...] = (own[start_of(ox, tok_rows), :] + orecv[ox].astype(jnp.float32)).astype(
-        jnp.bfloat16
-    )
+    fsend[...] = (total + orecv[ox].astype(jnp.float32)).astype(jnp.bfloat16)
     finish().start()
+    to_partner(x)
+    total = own[start_of(x, tok_rows), :] + last_part(c, x)
     own_pair(x).wait_recv()
     out_ref[:, mine] = (
-        tok[:, mine].astype(jnp.float32)
-        + own[start_of(x, tok_rows), :]
-        + orecv[x].astype(jnp.float32)
+        tok[:, mine].astype(jnp.float32) + total + orecv[x].astype(jnp.float32)
     ).astype(out_ref.dtype)
 
     for kind in (0, 1):

time: 113 us -> 113 us (level)
  no operation moved by 1% of the time
where the time goes in v6:
time: 113 us
  Pallas kernels  112 us (99%)
    pallas_call x1, Pallas kernels, fused(): pl.pallas_call(functools.partial(fused_kernel, (planes, chips, cores)), i...  112 us

profile of v6, /device:TPU:0, one launch (start us, length us, event | category | flops | bytes accessed | tf_op | source)
XLA Modules:
  0.0 112.7 jit_solution(11064714397495468633)
XLA Ops:
  0.0 112.0 %shard_map.73 = bf16[128,1536]{1,0:T(8,128)(2,1)S(1)} custom-call(bf16[128,1536]{1,0:T(8,128)(2,1)} %tok_hbm.1, s32[8,128]{1,0:T(8,128)} %bitcast.2, f32[8,128]{1,0:T(8,128)} %bitcast.3, bf16[16,384,768]{2,1,0:T(8,128)(2,1)} %win_hbm.1, bf16[16,768,384]{2,1,0:T(8,128)(2,1)} %wout_hbm.1, bf16[384,768]{1,0:T(8,128)(2,1)} %sin_hbm.1, bf16[768,384]{1,0:T(8,128)(2,1)} %sout_hbm.1), custom_call_target="tpu_custom_call" | custom-call | tf_op jit(solution)/shard_map/pallas_call | solution.py:731
  112.0 0.7 copy.9

commit v7 on v6

--- a/solution.py
+++ b/solution.py
@@ -241,6 +241,10 @@
     zrecv,
     fsend,
     frecv,
+    lsend,
+    lrecv,
+    lpick,
+    lscaled,
     isem,
     lsem,
     wssem,
@@ -263,6 +267,8 @@
     orsem,
     fssem,
     frsem,
+    lssem,
+    lrsem,
 ):
     planes, chips, cores = sizes
     dp = chips * cores
@@ -276,7 +282,8 @@
     own_rows = chips * tok_rows
     last = planes - 1
     head = min(HEAD, experts // 2)
-    close = max(experts - 1, head + 1)
+    close = experts - 2
+    piece = slots // cores
 
     z = lax.axis_index("expert")
     d = lax.axis_index("dp")
@@ -400,7 +407,10 @@
         return remote(ref, ref, s_sem.at[kind], zrsem.at[0, kind], partner)
 
     def swap(k, e):
-        return remote(send.at[k, e], recv.at[k, e], pssem.at[0], prsem.at[k, e], across)
+        return remote(send.at[k, e], recv.at[k, e], pssem.at[lax.div(k, last)], prsem.at[k, e], across)
+
+    def last_swap(e, g):
+        return remote(lsend.at[e, g], lrecv.at[e, g], lssem.at[0], lrsem.at[e, g], across)
 
     def shared_swap(b):
         return remote(ssend.at[b], srecv.at[b], ssem.at[0], srsem.at[b], across)
@@ -546,7 +556,15 @@
             partner_in(0).wait_recv()
             loop(0, head, project_and_send)
             partner_in(1).wait_recv()
-            loop(head, experts, project)
+            loop(head, close, project)
+            for e in range(close, experts):
+                pre = jnp.dot(rows[e], win[e], preferred_element_type=jnp.float32)
+                for g in range(cores):
+                    lanes = slice(g * own_rows, (g + 1) * own_rows)
+                    row = lax.broadcasted_iota(jnp.int32, (piece, own_rows), 0) + g * piece
+                    match = row == keys[e : e + 1, lanes]
+                    lpick[e - close, g] = jnp.where(match, 1.0, 0.0).astype(jnp.bfloat16)
+                    lsend[e - close, g] = pre[g * piece : (g + 1) * piece].astype(jnp.bfloat16)
         else:
             loop(0, experts, project_and_send)
 
@@ -600,7 +618,10 @@
 
         @pl.when(k == last - 1)
         def _():
-            loop(head, experts, lambda e: swap(last, e).start())
+            loop(head, close, lambda e: swap(last, e).start())
+            for g in range(cores):
+                for e in range(experts - close):
+                    last_swap(e, g).start()
 
         second_stage(k, turn, 0, experts)
         psend[k] = combine(turn, 0, experts, start_of(oc, own_rows), own_rows).astype(
@@ -620,30 +641,46 @@
     given().wait_recv()
     for r in range(1, planes):
         own[...] += zrecv[lax.rem(z + r, planes)].astype(jnp.float32)
-    second_stage(last, 2, close, experts)
-
-    def last_part(core, b):
-        lanes = start_of(core * chips + b, tok_rows)
-        return combine(2, close, experts, lanes, tok_rows)
-
-    def to_partner(b):
-        total = other[start_of(b, tok_rows), :] + last_part(oc, b)
-        osend[b] = total.astype(jnp.bfloat16)
-        own_pair(b).start()
-
     mine = start_of(x, half)
     theirs = start_of(ox, half)
-    to_partner(ox)
-    total = own[start_of(ox, tok_rows), :] + last_part(c, ox)
-    own_pair(ox).wait_recv()
-    fsend[...] = (total + orecv[ox].astype(jnp.float32)).astype(jnp.bfloat16)
-    finish().start()
-    to_partner(x)
-    total = own[start_of(x, tok_rows), :] + last_part(c, x)
+
+    def last_stage(g):
+        extra = None
+        for e in range(experts - close):
+            last_swap(e, g).wait_recv()
+            total = lsend[e, g].astype(jnp.float32) + lrecv[e, g].astype(jnp.float32)
+            h = jax.nn.gelu(total).astype(jnp.bfloat16)
+            result = jnp.dot(h, wout[close + e], preferred_element_type=jnp.float32)
+            gate = gslot[2, close + e, g * piece : (g + 1) * piece, :1]
+            lscaled[e, g] = (result * gate).astype(jnp.bfloat16)
+            part_sum = lax.dot_general(
+                lpick[e, g],
+                lscaled[e, g],
+                (((0,), (0,)), ((), ())),
+                preferred_element_type=jnp.float32,
+            )
+            extra = part_sum if extra is None else extra + part_sum
+
+        @pl.when(c != g)
+        def _():
+            other[...] += extra
+            for b in (ox, x):
+                osend[b] = other[start_of(b, tok_rows), :].astype(jnp.bfloat16)
+                own_pair(b).start()
+
+        @pl.when(c == g)
+        def _():
+            own[...] += extra
+            own_pair(ox).wait_recv()
+            total = own[start_of(ox, tok_rows), :] + orecv[ox].astype(jnp.float32)
+            fsend[...] = total.astype(jnp.bfloat16)
+            finish().start()
+
+    for g in range(cores):
+        last_stage(g)
     own_pair(x).wait_recv()
-    out_ref[:, mine] = (
-        tok[:, mine].astype(jnp.float32) + total + orecv[x].astype(jnp.float32)
-    ).astype(out_ref.dtype)
+    total = own[start_of(x, tok_rows), :] + orecv[x].astype(jnp.float32)
+    out_ref[:, mine] = (tok[:, mine].astype(jnp.float32) + total).astype(out_ref.dtype)
 
     for kind in (0, 1):
         token_swap(kind).wait_send()
@@ -653,7 +690,15 @@
     partner_shared_in().wait_send()
     partner_shared_out().wait_send()
     partner_out().wait_send()
-    remote(send, recv, pssem.at[0], prsem.at[0, 0], across).wait_send()
+    remote(send.at[pl.ds(0, last)], recv.at[pl.ds(0, last)], pssem.at[0], prsem.at[0, 0], across).wait_send()
+    remote(
+        send.at[last, pl.ds(0, close)],
+        recv.at[last, pl.ds(0, close)],
+        pssem.at[1],
+        prsem.at[0, 0],
+        across,
+    ).wait_send()
+    remote(lsend, lrecv, lssem.at[0], lrsem.at[0, 0], across).wait_send()
     remote(ssend, srecv, ssem.at[0], srsem.at[0], across).wait_send()
     remote(osend, orecv, bssem.at[0], brsem.at[0], partner).wait_send()
     remote(psend, precv, dssem.at[0], drsem.at[0], partner).wait_send()
@@ -708,6 +753,10 @@
         vmem((planes, own_rows, half), bf16),
         vmem((tok_rows, half), bf16),
         vmem((tok_rows, half), bf16),
+        vmem((2, cores, slots // cores, hidden), bf16),
+        vmem((2, cores, slots // cores, hidden), bf16),
+        vmem((2, cores, slots // cores, own_rows), bf16),
+        vmem((2, cores, slots // cores, half), bf16),
         dma((3,)),
         dma((4,)),
     ]
@@ -716,12 +765,13 @@
         ((2,), (2,)),
         ((2,), (planes, 2)),
         ((2,), (planes, 2)),
-        ((1,), (planes, experts)),
+        ((2,), (planes, experts)),
         ((1,), (chips,)),
         ((1,), (planes - 1,)),
         ((1,), (chips,)),
         ((1,), (1,)),
         ((1,), (1,)),
+        ((1,), (2, cores)),
     ]
     for sent, received in pairs:
         scratch += [dma(sent), dma(received)]

time: 113 us -> 112 us (level)
  Pallas kernels: 112 us -> 110 us
    pallas_call x1, Pallas kernels: 112 us -> 110 us  [fused(): pl.pallas_call(functools.partial(fused_kernel, (planes, chips, cores)), i...]
where the time goes in v7:
time: 112 us; the launch traced here: 111 us
  Pallas kernels  110 us (98%)
    pallas_call x1, Pallas kernels, fused(): pl.pallas_call(functools.partial(fused_kernel, (planes, chips, cores)), i...  110 us

profile of v7, /device:TPU:0, one launch (start us, length us, event | category | flops | bytes accessed | tf_op | source)
XLA Modules:
  0.0 110.9 jit_solution(15316115923307974697)
XLA Ops:
  0.0 110.1 %shard_map.73 = bf16[128,1536]{1,0:T(8,128)(2,1)S(1)} custom-call(bf16[128,1536]{1,0:T(8,128)(2,1)} %tok_hbm.1, s32[8,128]{1,0:T(8,128)} %bitcast.2, f32[8,128]{1,0:T(8,128)} %bitcast.3, bf16[16,384,768]{2,1,0:T(8,128)(2,1)} %win_hbm.1, bf16[16,768,384]{2,1,0:T(8,128)(2,1)} %wout_hbm.1, bf16[384,768]{1,0:T(8,128)(2,1)} %sin_hbm.1, bf16[768,384]{1,0:T(8,128)(2,1)} %sout_hbm.1), custom_call_target="tpu_custom_call" | custom-call | tf_op jit(solution)/shard_map/pallas_call | solution.py:781
  110.1 0.7 copy.9

commit v8 on v7

--- a/solution.py
+++ b/solution.py
@@ -269,6 +269,7 @@
     frsem,
     lssem,
     lrsem,
+    known,
 ):
     planes, chips, cores = sizes
     dp = chips * cores
@@ -433,9 +434,23 @@
         return remote(fsend, frecv, fssem.at[0], frsem.at[0], across)
 
     barrier = pltpu.get_barrier_semaphore()
-    peers = [{"expert": lax.rem(z + i, planes)} for i in range(1, planes)]
-    for device in [across, partner] + peers:
+    hops = (z > 0).astype(jnp.int32) + (z < last).astype(jnp.int32)
+
+    def greet(semaphore):
+        for move, there in ((-1, z > 0), (1, z < last)):
+
+            @pl.when(there)
+            def _():
+                pl.semaphore_signal(
+                    semaphore,
+                    inc=1,
+                    device_id={"expert": z + move},
+                    device_id_type=mesh_ids,
+                )
+
+    for device in (across, partner):
         pl.semaphore_signal(barrier, inc=1, device_id=device, device_id_type=mesh_ids)
+    greet(barrier)
     read_tok = pltpu.make_async_copy(tok_hbm, tok, isem.at[0])
     read_ids = pltpu.make_async_copy(ids_hbm, ids_in, isem.at[1])
     read_gate = pltpu.make_async_copy(gate_hbm, gate_in, isem.at[2])
@@ -443,9 +458,6 @@
     read_ids.start()
     read_gate.start()
     local_shared_in().start()
-    local_in().start()
-    local_shared_out().start()
-    local_out().start()
     read_ids.wait()
     read_gate.wait()
     meta[z, c * chips + x, :picks] = ids_in[...].astype(jnp.float32)
@@ -457,7 +469,11 @@
     norm[...] = (center * lax.rsqrt(spread + 1e-06)).astype(jnp.bfloat16)
     xall[z, c, x] = norm[:, start_of(x, half)]
 
-    pl.semaphore_wait(barrier, planes + 1)
+    local_in().start()
+    local_shared_out().start()
+    local_out().start()
+    pl.semaphore_wait(barrier, 2 + hops)
+    greet(known.at[0])
     for kind in (1, 0):
         token_swap(kind).start()
     partner_shared_in().start()
@@ -481,6 +497,10 @@
     partner_in(1).start()
     shared_first(ox)
     shared_swap(ox).start()
+    for step in range(1, last):
+        pl.semaphore_wait(known.at[step - 1], hops)
+        if step < last - 1:
+            greet(known.at[step])
 
     before = jnp.where(
         lax.broadcasted_iota(jnp.int32, (tok_rows, tok_rows), 0)
@@ -775,6 +795,7 @@
     ]
     for sent, received in pairs:
         scratch += [dma(sent), dma(received)]
+    scratch.append(pltpu.SemaphoreType.REGULAR((planes - 2,)))
     given = (tokens, expert_ids.T, gate_weights.T, expert_in, expert_out, shared_in, shared_out)
     given = [pltpu.with_memory_space_constraint(a, pltpu.HBM) for a in given]
     apart = pl.BlockSpec(memory_space=pl.ANY)
@@ -795,7 +816,7 @@
     tokens, expert_in = args[0], args[3]
     return (
         dp == 4
-        and 1 < planes <= 8
+        and planes == 4
         and expert_in.shape[0] // (mesh.shape["sweep"] * planes) % 2 == 0
         and expert_in.shape[0] // (mesh.shape["sweep"] * planes) <= 16
         and tokens.shape[0] // (mesh.shape["sweep"] * planes * dp) == 128

time: 112 us -> 111 us (level)
    pallas_call x1, Pallas kernels: 110 us -> 109 us  [fused(): pl.pallas_call(functools.partial(fused_kernel, (planes, chips, cores)), i...]
where the time goes in v8:
time: 111 us; the launch traced here: 110 us
  Pallas kernels  109 us (98%)
    pallas_call x1, Pallas kernels, fused(): pl.pallas_call(functools.partial(fused_kernel, (planes, chips, cores)), i...  109 us

profile of v8, /device:TPU:0, one launch (start us, length us, event | category | flops | bytes accessed | tf_op | source)
XLA Modules:
  0.0 109.6 jit_solution(6205950089114382111)
XLA Ops:
  0.0 108.8 %shard_map.73 = bf16[128,1536]{1,0:T(8,128)(2,1)S(1)} custom-call(bf16[128,1536]{1,0:T(8,128)(2,1)} %tok_hbm.1, s32[8,128]{1,0:T(8,128)} %bitcast.2, f32[8,128]{1,0:T(8,128)} %bitcast.3, bf16[16,384,768]{2,1,0:T(8,128)(2,1)} %win_hbm.1, bf16[16,768,384]{2,1,0:T(8,128)(2,1)} %wout_hbm.1, bf16[384,768]{1,0:T(8,128)(2,1)} %sin_hbm.1, bf16[768,384]{1,0:T(8,128)(2,1)} %sout_hbm.1), custom_call_target="tpu_custom_call" | custom-call | tf_op jit(solution)/shard_map/pallas_call | solution.py:802
  108.9 0.7 copy.9
